TPU v7x, 128 devices: a whole 4x4x4 slice. The times are simulated.
128 devices in a mesh: seq: 32 (over x, z, core), head: 4 (over y).
Axes of the slice: x: 4, y: 4, z: 4, core: 2. Of those that a mesh axis runs over, the one named last changes fastest.
Arguments:
- xs: bfloat16 [32768, 4096], P('seq', 'head'), may hold values from -6 to 6
- gate_branch: bfloat16 [32768, 4096], P('seq', 'head'), may hold values from -6 to 6
- bmat: bfloat16 [32768, 128], P('seq'), may hold values from -0.25 to 0.25
- cmat: bfloat16 [32768, 128], P('seq'), may hold values from -0.25 to 0.25
- dt_code: int32 [64, 32768], P('head', 'seq'), may hold values from 1 to 131072
- resets: int32 [32768], P('seq'), may hold values 0 or 1
- decay_rate: float32 [64], P('head'), may hold values from 1.2207031e-05 to 0.08, as said below
- skip: float32 [64], P('head'), may hold values from 0.5 to 1.5
- norm_gain: float32 [4096], P('head'), may hold values from 0.1 to 1.9
- out_weight: bfloat16 [4096, 4096], P('head'), may hold values from -0.09375 to 0.09375
Outputs:
- mixed: bfloat16 [32768, 4096], P(('seq', 'head'))
Inputs may be any that keep to these rules, and one draw needn't show every extreme that they name: `decay_rate`: positive rates.
All inputs are finite; a program needn't handle non-finite values. No bound on the sum of `resets` on one device may be relied on, other than what follows from the above.
Results may differ from a plain program's by a relative error of at most 0.023.
Values may be sent and summed in bfloat16 or wider, within the bound.
A program may use at most 128 MiB of HBM per device.

v0:
```python
import jax
import jax.numpy as jnp
from jax import lax
from jax.sharding import PartitionSpec as P

HEAD_DIM = 64
STATE = 128
SPAN = 256
INNER = 4096


def laid_out(tiles, dim):
    shape = list(tiles.shape[1:])
    shape[dim] *= tiles.shape[0]
    return jnp.moveaxis(tiles, 0, dim).reshape(shape)


def copy_for_each(array, axis):
    copies = jnp.broadcast_to(array, (lax.axis_size(axis), *array.shape))
    return lax.all_to_all(copies, axis, split_axis=0, concat_axis=0, tiled=True)


def gathered_copies(array, axis, dim):
    return laid_out(copy_for_each(array, axis), dim)


def over_copies(array, axis):
    everything = copy_for_each(array, axis)
    return jnp.sum(everything, axis=0)


def local(xs, gate_branch, bmat, cmat, dt_code, resets, decay_rate, skip, norm_gain, out_weight):
    tokens_here = xs.shape[0]
    local_heads = dt_code.shape[0]
    blocks = tokens_here // SPAN
    step_size = dt_code.astype(jnp.float32) / 16.0
    input_scale = jnp.minimum(step_size, 1.0)
    logarithmic_damping = -decay_rate[:, None] * step_size
    cumulative = jnp.cumsum(logarithmic_damping.reshape(local_heads, blocks, SPAN), axis=2)
    counts = jnp.cumsum(resets.reshape(blocks, SPAN), axis=1)
    position = jnp.arange(SPAN)
    linked = (counts[:, :, None] == counts[:, None, :]) & (position[None, :] <= position[:, None])[
        None
    ]
    gaps = jnp.where(linked[None], cumulative[:, :, :, None] - cumulative[:, :, None, :], 0.0)
    within = jnp.where(linked[None], jnp.exp(gaps), 0.0)
    key_blocks = bmat.reshape(blocks, SPAN, STATE)
    query_blocks = cmat.reshape(blocks, SPAN, STATE)
    intersection = jnp.einsum(
        "cin,cjn->cij", query_blocks, key_blocks, preferred_element_type=jnp.float32
    )
    raw_values = xs.reshape(blocks, SPAN, local_heads, HEAD_DIM)
    step_scale = input_scale.reshape(local_heads, blocks, SPAN).transpose(1, 2, 0)[:, :, :, None]
    scaled = (raw_values.astype(jnp.float32) * step_scale).astype(jnp.bfloat16)
    scores = (within * intersection[None]).astype(jnp.bfloat16)
    intra = jnp.einsum("hcij,cjhp->cihp", scores, scaled, preferred_element_type=jnp.float32)
    to_end = jnp.where(
        counts[None] == counts[None, :, -1:], jnp.exp(cumulative[:, :, -1:] - cumulative), 0.0
    )
    through = jnp.where(counts[None, :, -1] == 0, jnp.exp(cumulative[:, :, -1]), 0.0)
    from_start = jnp.where(counts[None] == 0, jnp.exp(cumulative), 0.0)
    weighted = (scaled.astype(jnp.float32) * to_end.transpose(1, 2, 0)[:, :, :, None]).astype(
        jnp.bfloat16
    )
    fresh = jnp.einsum("cjhp,cjn->chpn", weighted, key_blocks, preferred_element_type=jnp.float32)
    starts = []
    attained_limit = []
    running = jnp.zeros((local_heads, HEAD_DIM, STATE), jnp.float32)
    product = jnp.ones((local_heads,), jnp.float32)
    for block in range(blocks):
        starts.append(running)
        attained_limit.append(product)
        running = through[:, block, None, None] * running + fresh[block]
        product = product * through[:, block]
    local_starts = jnp.stack(starts)
    reach = jnp.stack(attained_limit, axis=0)
    query_float = query_blocks.astype(jnp.float32)
    start_weight = from_start.transpose(1, 2, 0)[:, :, :, None]
    decays = gathered_copies(product[None], "seq", 0)
    shard_count = decays.shape[0]
    rank = lax.axis_index("seq")
    shard_ids = jnp.arange(shard_count)
    between = (shard_ids[None, :] > shard_ids[:, None]) & (shard_ids[None, :] < rank)
    factors = jnp.where(between[:, :, None], decays[None, :, :], 1.0)
    weights = jnp.prod(factors, axis=1) * (shard_ids < rank).astype(jnp.float32)[:, None]
    empty = jnp.zeros((local_heads, HEAD_DIM, STATE), jnp.float32)
    incoming = empty + jnp.einsum(
        "jh,jhpn->hpn",
        weights,
        lax.all_gather(running[None].astype(jnp.bfloat16), "seq", axis=0, tiled=True).astype(
            jnp.float32
        ),
    )
    full_starts = local_starts + reach[:, :, None, None] * incoming[None]
    inter = jnp.einsum("cin,chpn->cihp", query_float, full_starts) * start_weight
    result = intra + inter + skip[None, None, :, None] * raw_values.astype(jnp.float32)
    ssm_out = result.reshape(tokens_here, local_heads * HEAD_DIM)
    gated = ssm_out * jax.nn.silu(gate_branch.astype(jnp.float32))
    squared_values = over_copies(jnp.sum(gated * gated, axis=1), "head")
    hidden = (
        gated * lax.rsqrt(squared_values[:, None] / INNER + 1e-05) * norm_gain[None, :]
    ).astype(jnp.bfloat16)
    return lax.psum_scatter(
        jnp.dot(hidden, out_weight, preferred_element_type=jnp.float32).astype(jnp.bfloat16),
        "head",
        scatter_dimension=0,
        tiled=True,
    )


def solution(mesh):
    in_specs = (
        P("seq", "head"),
        P("seq", "head"),
        P("seq", None),
        P("seq", None),
        P("head", "seq"),
        P("seq"),
        P("head"),
        P("head"),
        P("head"),
        P("head", None),
    )
    out_specs = P(("seq", "head"), None)
    return jax.shard_map(local, mesh=mesh, in_specs=in_specs, out_specs=out_specs, check_vma=False)
```

profile of v0, /device:TPU:1, one launch (start us, length us, event | category | flops | bytes accessed | tf_op | source)
XLA Modules:
  0.0 221.5 jit_solution(469861393949509312)
XLA Ops:
  6.5 0.7 negate_multiply_fusion
  7.2 0.9 multiply_minimum_fusion
  8.2 0.1 reshape.251
  8.2 2.3 %reduce-window.16 = f32[16,4,2,128]{3,0,1,2:T(8,128)S(1)} reduce-window(f32[16,4,2,128]{3,0,1,2:T(8,128)S(1)} %copy.74, f32[]{:T(128)} %constant.12.clone.1), window={size=1x1x1x128 pad=0_0x0_0x0_0x127_0}, to_apply=%region_2.3 | reduce-window | flops 2080768 | bytes 131076 | tf_op jit(solution)/shard_map/reduce-window.2
  10.5 0.2 slice_reduce_fusion
  10.7 0.1 copy_bitcast_fusion
  10.8 0.2 slice_reduce_fusion.1
  11.0 2.3 %reduce-window.14 = s32[4,2,128]{2,1,0:T(2,128)S(1)} reduce-window(s32[4,2,128]{2,1,0:T(2,128)} %bitcast.109, s32[]{:T(128)} %constant.11.clone.1), window={size=1x1x128 pad=0_0x0_0x127_0}, to_apply=%region_0.0 | reduce-window | flops 130048 | bytes 8196 | tf_op jit(solution)/shard_map/reduce-window
  13.2 0.1 slice.62
  13.3 0.1 copy.72
  13.5 0.1 copy.73
  13.6 0.1 add_bitcast_fusion.1
  13.6 0.1 slice.65
  13.7 0.1 copy.91
  13.8 0.1 exponential_select_fusion
  13.9 0.1 broadcast_compare_fusion
  14.0 0.1 select_bitcast_fusion
  14.1 4.1 %copy.71 = f32[1024,1024]{0,1:T(8,128)} copy(bf16[1024,1024]{1,0:T(8,128)(2,1)} %param.10) | data formatting | bytes 6291456 | tf_op jit(solution)/shard_map/convert_element_type | solution.py:54
  18.3 5.6 %reshape.256 = f32[4,256,16,64]{1,0,3,2:T(4,128)} reshape(f32[1024,1024]{0,1:T(8,128)} %copy.71) | data formatting | bytes 8388608 | tf_op jit(solution)/shard_map/convert_element_type | solution.py:54
  23.9 4.9 %multiply_convert_fusion.3 = (bf16[4,256,16,64]{1,0,3,2:T(4,128)(2,1)S(1)}, bf16[4,256,16,64]{1,0,3,2:T(4,128)(2,1)}) fusion(f32[4,256,16]{1,0,2:T(4,128)S(1)} %copy.78, f32[4,256,16,64]{1,0,3,2:T(4,128)} %reshape.256, f32[4,256,16]{1,0,2:T(4,128)S(1)} %bitcast.104), kind=kLoop, calls=%fused_computation.22 | loop fusion | flops 5242880 | bytes 8519680 | tf_op jit(solution)/shard_map/convert_element_type | solution.py:62
  28.9 0.7 fusion.20
  29.6 1.1 fusion.29
  30.7 0.6 broadcast_in_dim.114
  31.3 9.4 %all-to-all-start = ((f32[32,1,16]{2,1,0:T(1,128)}), f32[32,1,16]{2,1,0:T(1,128)S(1)}, u32[]{:S(2)}, u32[]{:S(2)}) async-start(f32[32,1,16]{2,1,0:T(1,128)} %broadcast_in_dim.114), calls=%async_computation | async-start | bytes 32768 | tf_op jit(solution)/shard_map/all_to_all | solution.py:20
  40.8 0.6 pad_maximum_fusion
  41.4 0.6 fusion.30
  42.0 0.9 compare_and_fusion
  43.0 1.4 fusion.38
  44.3 0.6 fusion.35
  44.9 0.6 pad.4.clone
  45.5 3.0 %copy.83 = bf16[1024,1024]{0,1:T(8,128)(2,1)S(1)} copy(bf16[1024,1024]{1,0:T(8,128)(2,1)} %param.11) | data formatting | bytes 4194304 | tf_op args[1]
  48.6 0.7 copy.80
  49.2 1.3 select_reduce_fusion
  50.5 0.7 multiply_bitcast_fusion
  51.3 0.1 copy.86
  51.4 35.9 %all-gather.2.cloned.1.call-done = bf16[32,16,64,128]{3,2,1,0:T(8,128)(2,1)} async-done(((bf16[1,16,64,128]{3,2,1,0:T(8,128)(2,1)}), bf16[32,16,64,128]{3,2,1,0:T(8,128)(2,1)}) %all-gather.2.cloned.1.call-update) | async-done | bytes 8388624 | tf_op jit(solution)/shard_map/all_gather | solution.py:90
  87.3 8.2 %fusion.1 = f32[16,1,64,128]{3,1,2,0:T(1,128)S(1)} fusion(bf16[32,16,1,1]{0,2,3,1:T(2,128)(2,1)S(1)} %copy.86, bf16[32,16,64,128]{3,2,1,0:T(8,128)(2,1)} %all-gather.2.cloned.1.call-done), kind=kOutput, calls=%fused_computation.2 | convolution fusion | flops 8388608 | bytes 8913920 | tf_op jit(solution)/shard_map/jh,jhpn->hpn/dot_general | solution.py:87
  95.6 0.8 fusion.14
  96.3 1.4 copy-done.2
  97.7 0.7 copy-done.5
  98.4 5.6 %fusion.13 = f32[4,256,16,64]{1,3,2,0:T(8,128)S(1)} fusion(f32[4,16,64,256]{3,2,1,0:T(8,128)S(1)} %fusion.14, f32[4,256,16,64]{1,0,3,2:T(4,128)S(1)} %copy-done.2, f32[4,256,256]{2,1,0:T(8,128)S(1)} %copy-done.6, f32[16,4,256]{2,0,1:T(8,128)S(1)} %copy_bitcast_fusion, pred[4,256,256]{2,1,0:T(8,128)(4,1)S(1)} %copy-done.8, ...), kind=kOutput, calls=%fused_computation.18 | convolution fusion | flops 562036736 | bytes 16121920 | tf_op jit(solution)/shard_map/hcij,cjhp->cihp/dot_general | solution.py:56
  104.0 3.0 %copy.82 = f32[4,256,16,64]{1,0,3,2:T(4,128)S(1)} copy(f32[4,256,16,64]{1,3,2,0:T(8,128)S(1)} %fusion.13) | data formatting | bytes 8388608 | tf_op jit(solution)/shard_map/add | solution.py:96
  107.0 1.0 copy.94
  108.1 2.0 copy-done.3
  110.0 1.3 multiply_reduce_fusion
  111.4 8.0 %all_to_all.11 = f32[4,1,1024]{2,1,0:T(1,128)S(1)} all-to-all(f32[4,1,1024]{2,1,0:T(1,128)S(1)} %broadcast_in_dim.119), channel_id=1, replica_groups=mesh['seq'=32,'head'=4] {'head'}, dimensions={0} | all-to-all | bytes 32768 | tf_op jit(solution)/shard_map/all_to_all | solution.py:20
  119.4 15.9 %convolution_convert_fusion = bf16[1024,4096]{1,0:T(8,128)(2,1)} fusion(bf16[1024,4096]{1,0:T(8,128)(2,1)} %param.19, f32[1024]{0:T(1024)S(1)} %copy-done.11, f32[1024]{0:T(1024)S(1)} %add_rsqrt_fusion, f32[1024,1024]{0,1:T(8,128)} %bitcast.99, bf16[1024,1024]{0,1:T(8,128)(2,1)S(1)} %copy.83), kind=kOutput, calls=%fused_computation.9 | convolution fusion | flops 8603566080 | bytes 23076864 | tf_op jit(solution)/shard_map/dot_general | solution.py:104
  135.4 79.3 %reduce-scatter.2.cloned.1.call-done = bf16[256,4096]{1,0:T(8,128)(2,1)} async-done(((bf16[1024,4096]{1,0:T(8,128)(2,1)}), bf16[256,4096]{1,0:T(8,128)(2,1)}) %reduce-scatter.2.cloned.1.call-update) | async-done | bytes 2097168 | tf_op jit(solution)/shard_map/reduce_scatter | solution.py:103
  (46 shorter events, 0.4 us)
Async XLA Ops:
  6.5 36.4 %copy-start = (bf16[1024,128]{1,0:T(8,128)(2,1)S(1)}, bf16[1024,128]{1,0:T(8,128)(2,1)}, u32[]{:S(2)}) copy-start(bf16[1024,128]{1,0:T(8,128)(2,1)} %param.13) | copy-start | bytes 786436
  6.5 80.7 %all-gather.2.cloned.1.call-start = ((), (), s32[]{:S(2)}) async-start(), calls=%async_computation.3 | async-start | bytes 8650752 | tf_op jit(solution)/shard_map/all_gather | solution.py:90
  23.9 4.9 %copy-start.7 = (bf16[1024,128]{1,0:T(8,128)(2,1)S(1)}, bf16[1024,128]{1,0:T(8,128)(2,1)}, u32[]{:S(2)}) copy-start(bf16[1024,128]{1,0:T(8,128)(2,1)} %param.12) | copy-start | bytes 786436
  31.3 17.3 %all-to-all-start = ((f32[32,1,16]{2,1,0:T(1,128)}), f32[32,1,16]{2,1,0:T(1,128)S(1)}, u32[]{:S(2)}, u32[]{:S(2)}) async-start(f32[32,1,16]{2,1,0:T(1,128)} %broadcast_in_dim.114), calls=%async_computation | async-start | bytes 32768 | tf_op jit(solution)/shard_map/all_to_all | solution.py:20
  40.7 174.0 %reduce-scatter.2.cloned.1.call-start = ((), (), s32[]{:S(2)}) async-start(), calls=%async_computation.4 | async-start | bytes 10485760 | tf_op jit(solution)/shard_map/reduce_scatter | solution.py:103
  51.4 44.2 %copy-start.9 = (f32[4,16]{1,0:T(4,128)S(1)}, f32[4,16]{1,0:T(4,128)}, u32[]{:S(2)}) copy-start(f32[4,16]{1,0:T(4,128)} %pad_maximum_fusion) | copy-start | bytes 772
  51.4 44.2 %copy-start.10 = (f32[4]{0:T(128)S(1)}, f32[4]{0:T(128)}, u32[]{:S(2)}) copy-start(f32[4]{0:T(128)} %pad.4.clone) | copy-start | bytes 52
  87.3 8.3 %copy-start.4 = (f32[1,16,64,128]{3,2,1,0:T(8,128)S(1)}, f32[1,16,64,128]{3,2,1,0:T(8,128)}, u32[]{:S(2)}) copy-start(f32[1,16,64,128]{3,2,1,0:T(8,128)} %get-tuple-element.10) | copy-start | bytes 1572868
  87.3 9.1 %copy-start.6 = (f32[4,256,256]{2,1,0:T(8,128)S(1)}, f32[4,256,256]{2,1,0:T(8,128)}, u32[]{:S(2)}) copy-start(f32[4,256,256]{2,1,0:T(8,128)} %fusion.38) | copy-start | bytes 3145732
  95.5 2.2 copy-start.2
  95.5 2.9 %copy-start.5 = (bf16[4,256,16,64]{1,0,3,2:T(4,128)(2,1)S(1)}, bf16[4,256,16,64]{1,0,3,2:T(4,128)(2,1)}, u32[]{:S(2)}) copy-start(bf16[4,256,16,64]{1,0,3,2:T(4,128)(2,1)} %get-tuple-element.12) | copy-start | bytes 6291460
  95.5 2.9 %copy-start.8 = (pred[4,256,256]{2,1,0:T(8,128)(4,1)S(1)}, pred[4,256,256]{2,1,0:T(8,128)(4,1)}, u32[]{:S(2)}) copy-start(pred[4,256,256]{2,1,0:T(8,128)(4,1)} %compare_and_fusion) | copy-start | bytes 786436
  95.5 2.9 %copy-start.12 = (f32[16]{0:T(128)S(1)}, f32[16]{0:T(128)}, u32[]{:S(2)}) copy-start(f32[16]{0:T(128)} %param.17) | copy-start | bytes 196
  108.1 2.0 copy-start.3
  108.1 11.4 %copy-start.11 = (f32[1024]{0:T(1024)S(1)}, f32[1024]{0:T(1024)}, u32[]{:S(2)}) copy-start(f32[1024]{0:T(1024)} %param.18) | copy-start | bytes 12292
  135.4 79.3 %copy-start.1 = (bf16[1024,128]{1,0:T(8,128)(2,1)S(1)}, bf16[1024,128]{1,0:T(8,128)(2,1)}, u32[]{:S(2)}) copy-start(bf16[1024,128]{1,0:T(8,128)(2,1)} %param.13) | copy-start | bytes 786436
Sparse Core Ops, SparseCore 0:
  30.8 56.4 all-gather.1
  135.5 79.1 reduce-scatter.1
where the time goes:
time: 222 us
  waiting for transfers between devices  115 us (52%)
  matrix products  32.6 us (15%)
  local copies, waits for them, and re-layouts  23.8 us (11%)
  other arithmetic  18.8 us (8%)
  between operations  13.7 us (6%)
  starting transfers between devices  9.46 us (4%)
  blocking collectives  8.02 us (4%)
    reduce_scatter x1, waiting for transfers between devices, local(): lax.psum_scatter(jnp.dot(hidden, out_weight, preferred_element_type=jnp.f...  79.3 us
    all_gather x1, waiting for transfers between devices, local(): lax.all_gather(running[None].astype(jnp.bfloat16), 'seq', axis=0, tiled=T...  35.9 us
    dot_general x1, matrix products, local(): jnp.dot(hidden, out_weight, preferred_element_type=jnp.float32)  15.9 us
    convert_element_type x2, local copies, waits for them, and re-layouts, local(): scaled = (raw_values.astype(jnp.float32) * step_scale).astype(jnp.bfloat16)  9.74 us
    all_to_all x1, starting transfers between devices, copy_for_each(): return lax.all_to_all(copies, axis, split_axis=0, concat_axis=0, tiled=True)  9.42 us
    dot_general x1, matrix products, local(): jnp.einsum('jh,jhpn->hpn', weights, lax.all_gather(running[None].astype(j...  8.24 us
    unnamed x30, local copies, waits for them, and re-layouts  8.19 us
    all_to_all x1, blocking collectives, copy_for_each(): return lax.all_to_all(copies, axis, split_axis=0, concat_axis=0, tiled=True)  8.02 us
  transfers between devices with their start and end apart: 3, of which 2 were waited for; matrix products, arithmetic and copies ran while one was open for 5% of the time, Pallas kernels for 0%

commit v1 on v0

v1 whole, which is shorter than its diff:
```python
import jax
import jax.numpy as jnp
from jax import lax
from jax.experimental import pallas as pl
from jax.experimental.pallas import tpu as pltpu
from jax.sharding import PartitionSpec as P

HEAD_DIM = 64
STATE = 128
SPAN = 256
INNER = 4096
MESH = pl.DeviceIdType.MESH
LOG2E = 1.4426950408889634
F32 = jnp.float32
BF16 = jnp.bfloat16

WIDTHS = (384, 384, 512)
DIRECT = 512
DIRECT_PIECES = 4


def iota(shape, dim):
    return lax.broadcasted_iota(jnp.int32, shape, dim)


def kernel(
    xs_hbm, gate_hbm, bmat, cmat, dt, resets, gain, w_hbm, rate, skip,
    out_hbm,
    xs, gate, weight, hid, hid_send, sums, sums_send, acc, out_buf,
    tri, col, split, bt, cjp, cntrow, grow, starts, reach, chunk_send, chunk_recv, inc_send, inc_recv,
    cbm, local,
    in_sem, own_sem, slice_ss, slice_rs, direct_ss, direct_rs, step_ss, step_rs,
    chunk_ss, chunk_rs, inc_ss, inc_rs, hid_ss, hid_rs, sum_ss, sum_rs, fwd_ss, fwd_rs, fsum_ss, fsum_rs,
    out_ss, out_rs, out_sem,
):
    s = lax.axis_index("seq")
    h = lax.axis_index("head")
    x, z, c = s // 8, (s // 2) % 4, s % 2
    other = (s + 1 - 2 * c, h)

    def remote(src, dst, ss, rs, dev):
        return pltpu.make_async_remote_copy(
            src_ref=src, dst_ref=dst, send_sem=ss, recv_sem=rs, device_id=dev, device_id_type=MESH
        )

    copies_in = [
        pltpu.make_async_copy(xs_hbm, xs, in_sem.at[0]),
        pltpu.make_async_copy(gate_hbm, gate, in_sem.at[1]),
    ]
    for cp in copies_in:
        cp.start()

    barrier = pltpu.get_barrier_semaphore()

    @pl.loop(1, 32)
    def _(i):
        pl.semaphore_signal(barrier, inc=1, device_id=((s + i) % 32, h), device_id_type=MESH)

    for d in (1, 2, 3):
        pl.semaphore_signal(barrier, inc=1, device_id=(s, (h + d) % 4), device_id_type=MESH)

    planes = [(h + 1) % 4, (h + 3) % 4, (h + 2) % 4]
    arrives_as = (1, 0, 2)

    px, pz = x % 2, z % 2
    ax, az = x // 2, z // 2
    bx, bz = ((x + 1) // 2) % 2, ((z + 1) // 2) % 2
    x_a, z_a = x + 1 - 2 * px, z + 1 - 2 * pz
    x_b, z_b = (x + 3 + 2 * px) % 4, (z + 3 + 2 * pz) % 4

    def at(xx, zz):
        return ((xx * 4 + zz) * 2 + c, h)

    along = (at(x_a, z), at(x, z_a), at(x_b, z), at(x, z_b))
    bits = ((px, pz, ax, az), (pz, px, az, bx), (px, pz, bx, bz), (pz, px, bz, ax))
    mine = [b0 + 2 * b1 + 4 * b2 + 8 * b3 for b0, b1, b2, b3 in bits]
    base = c * 2048

    def slice_copy(j, k):
        rows = pl.ds(pl.multiple_of(mine[k] * 64, 64), 64)
        width = WIDTHS[arrives_as[j]]
        src = w_hbm.at[rows, pl.ds(pl.multiple_of(base + k * width, 128), width)]
        dst = weight.at[h, rows, pl.ds(k * width, width)]
        return remote(src, dst, slice_ss.at[j, k], slice_rs.at[arrives_as[j], k], (s, planes[j]))

    def slice_wait(j, k):
        rows = pl.ds(pl.multiple_of(mine[k] * 64, 64), 64)
        part = weight.at[planes[j], rows, pl.ds(k * WIDTHS[j], WIDTHS[j])]
        remote(part, part, slice_ss.at[j, k], slice_rs.at[j, k], (s, planes[j])).wait_recv()

    per = 1024 // DIRECT_PIECES

    def direct_copy(j, m):
        rows = pl.ds(m * per, per)
        src = w_hbm.at[rows, pl.ds(pl.multiple_of(base + 2048 - DIRECT, 128), DIRECT)]
        dst = weight.at[h, rows, pl.ds(2048 - DIRECT, DIRECT)]
        return remote(src, dst, direct_ss.at[j, m], direct_rs.at[1 - j, m], (s, planes[j]))

    def direct_wait(j, m):
        part = weight.at[planes[j], pl.ds(m * per, per), pl.ds(2048 - DIRECT, DIRECT)]
        remote(part, part, direct_ss.at[j, m], direct_rs.at[j, m], (s, planes[j])).wait_recv()

    def step_copy(t, j, k):
        first = (mine[k] // (1 << t)) * (64 << t)
        rows = pl.ds(pl.multiple_of(first, 64 << t), 64 << t)
        part = weight.at[planes[j], rows, pl.ds(k * WIDTHS[j], WIDTHS[j])]
        return remote(part, part, step_ss.at[t, j, k], step_rs.at[t, j, k], along[(k + t) % 4])

    own_weight = pltpu.make_async_copy(w_hbm.at[:, pl.ds(pl.multiple_of(base, 128), 2048)], weight.at[h], own_sem)
    own_weight.start()

    pl.semaphore_wait(barrier, 34)

    for j in (0, 1, 2):
        for k in range(4):
            slice_copy(j, k).start()

    tri[...] = jnp.where(iota((SPAN, SPAN), 0) <= iota((SPAN, SPAN), 1), 1.0, 0.0).astype(BF16)
    head_row = iota((16, SPAN), 0)
    slope = jnp.zeros((16, SPAN), F32)
    for n in range(16):
        slope = jnp.where(head_row == n, rate[n] * (-LOG2E / 16.0), slope)
    for b in range(4):
        d = dt[:, b * SPAN:(b + 1) * SPAN]
        flags = jnp.broadcast_to(resets[:, b * SPAN:(b + 1) * SPAN], (16, SPAN))
        parts = [d & 0xFF, d & 0xFF00, d & 0x30000, flags]
        stack = jnp.concatenate([p.astype(F32) for p in parts], axis=0).astype(BF16)
        run = jnp.dot(stack, tri[...], preferred_element_type=F32)
        c2 = (run[0:16] + run[16:32] + run[32:48]) * slope
        count = run[48:64]
        ls = jnp.log(jnp.minimum(d.astype(F32) * 0.0625, 1.0)) * LOG2E
        c2_end, count_end = c2[:, SPAN - 1:SPAN], count[:, SPAN - 1:SPAN]
        from_start = jnp.where(count == 0, jnp.exp2(c2), 0.0)
        to_end = jnp.where(count == count_end, jnp.exp2(c2_end - c2 + ls), 0.0)
        cjp[b] = c2 - ls
        cntrow[b] = count[0:8]
        table = jnp.concatenate([c2, from_start, to_end, count, jnp.zeros((64, SPAN), F32)], axis=0)
        flipped = table.T
        col[b] = flipped
        high = flipped.astype(BF16)
        low = (flipped - high.astype(F32)).astype(BF16)
        split[b] = jnp.concatenate([high, low], axis=1)
        bt[b] = bmat[b * SPAN:(b + 1) * SPAN, :].T

    copies_in[0].wait()

    @pl.loop(0, 8)
    def _(q):
        lanes = pl.ds(pl.multiple_of(q * 128, 128), 128)
        row, lane = iota((SPAN, SPAN), 0) % 128, iota((SPAN, SPAN), 1)
        pick = jnp.where(lane < 128, 16, 32) + 2 * q + (lane % 128) // 64
        pick = jnp.where(row == pick, 1.0, 0.0).astype(BF16)
        run = jnp.zeros((STATE, 128), F32)
        product = jnp.ones((1, 128), F32)
        for b in range(4):
            rows = pl.ds(b * SPAN, SPAN)
            wide = jnp.dot(split[b], pick, preferred_element_type=F32)
            grow[rows, lanes] = wide[:, 0:128]
            weighted = (xs[rows, lanes].astype(F32) * wide[:, 128:256]).astype(BF16)
            fresh = jnp.dot(bt[b], weighted, preferred_element_type=F32)
            starts[b, q] = run
            reach[b, q] = jnp.broadcast_to(product, (8, 128))
            through = wide[SPAN - 1:SPAN, 0:128]
            run = through * run + fresh
            product = product * through
        high = product.astype(BF16).astype(F32)
        rest = product - high
        mid = rest.astype(BF16).astype(F32)
        low = rest - mid
        line = iota((16, 128), 0)
        tail = jnp.where(line == 0, high, jnp.where(line == 1, mid, jnp.where(line == 2, low, 0.0))).astype(BF16)
        for r in range(4):
            chunk_send[q * 4 + r, 0:32, :] = run[r * 32:(r + 1) * 32].astype(BF16)
            chunk_send[q * 4 + r, 32:48, :] = tail

    def chunk_copy(i):
        o = (s + i) % 32
        return remote(chunk_send.at[o], chunk_recv.at[s], chunk_ss.at[i], chunk_rs.at[i], (o, h))

    @pl.loop(1, 32)
    def _(i):
        chunk_copy(i).start()

    chunk_recv[s] = chunk_send[s]

    half = SPAN // 2

    def inside(b):
        rows = pl.ds(pl.multiple_of(b * SPAN, SPAN), SPAN)
        table = col[b]
        pair = jnp.dot(cmat[rows, :], bt[b], preferred_element_type=F32)
        same = (table[:, 48:49] == cntrow[b][0:1, :]) & (iota((SPAN, SPAN), 1) <= iota((SPAN, SPAN), 0))
        cbm[...] = jnp.where(same, pair, 0.0)
        first = iota((SPAN, 128), 1) < HEAD_DIM
        for q in range(8):
            lanes = slice(q * 128, (q + 1) * 128)
            value = xs[rows, lanes]
            value_float = value.astype(F32)
            sides = (jnp.where(first, value_float, 0.0).astype(BF16), jnp.where(first, 0.0, value_float).astype(BF16))
            total = [jnp.where(first[0:half], skip[2 * q], skip[2 * q + 1]) * value_float[r * half:(r + 1) * half] for r in (0, 1)]
            for e in (0, 1):
                n = 2 * q + e
                ci = table[:, n:n + 1]
                cj = cjp[b, n:n + 1, :]
                for r in (0, 1):
                    lo, hi = r * half, (r + 1) * half
                    gap = jnp.minimum(ci[lo:hi] - cj[:, 0:hi], 0.0)
                    score = (jnp.exp2(gap) * cbm[lo:hi, 0:hi]).astype(BF16)
                    total[r] = total[r] + jnp.dot(score, sides[e][0:hi], preferred_element_type=F32)
            for r in (0, 1):
                local[pl.ds(pl.multiple_of(b * SPAN + r * half, half), half), lanes] = total[r]

    for j in (0, 1):
        for k in range(4):
            slice_wait(j, k)
            step_copy(0, j, k).start()

    pl.loop(0, 2)(inside)

    @pl.loop(1, 32)
    def _(i):
        chunk_copy(i).wait_recv()

    def scan(t, incoming):
        inc_send[t] = incoming.astype(BF16)
        tail = chunk_recv[t, 32:48, :].astype(F32)
        through = tail[0:1] + tail[1:2] + tail[2:3]
        return through * incoming + chunk_recv[t, 0:32, :].astype(F32)

    lax.fori_loop(0, 32, scan, jnp.zeros((32, 128), F32))

    def inc_copy(i):
        o = (s + i) % 32
        return remote(inc_send.at[o], inc_recv.at[s], inc_ss.at[i], inc_rs.at[i], (o, h))

    @pl.loop(1, 32)
    def _(i):
        inc_copy(i).start()

    inc_recv[s] = inc_send[s]

    for k in range(4):
        slice_wait(2, k)
        step_copy(0, 2, k).start()
    for j in (0, 1):
        for m in range(DIRECT_PIECES // 2):
            direct_copy(j, m).start()
    for j in (0, 1, 2):
        for k in range(4):
            step_copy(0, j, k).wait_recv()
            step_copy(1, j, k).start()

    pl.loop(2, 4)(inside)

    @pl.loop(1, 32)
    def _(i):
        inc_copy(i).wait_recv()

    copies_in[1].wait()

    def finish(b, put):
        rows = pl.ds(pl.multiple_of(b * SPAN, SPAN), SPAN)
        query = cmat[rows, :]

        def part(q, squares):
            lanes = pl.ds(pl.multiple_of(q * 128, 128), 128)
            incoming = inc_recv[pl.ds(q * 4, 4)].reshape(STATE, 128).astype(F32)
            state = (starts[b, q] + reach[b, q, 0:1, :] * incoming).astype(BF16)
            inter = jnp.dot(query, state, preferred_element_type=F32)
            value = local[rows, lanes] + grow[rows, lanes] * inter
            v = gate[rows, lanes].astype(F32)
            gated = value * (v / (1.0 + jnp.exp(-v)))
            put(lanes, (gated * gain[:, lanes]).astype(BF16))
            return squares + gated * gated

        squares = lax.fori_loop(0, 8, part, jnp.zeros((SPAN, 128), F32))
        total = jnp.broadcast_to(jnp.sum(squares, axis=1, keepdims=True), (SPAN, 128)).T[0:16, :]
        high = total.astype(BF16).astype(F32)
        return jnp.where(iota((16, SPAN), 0) == 0, high, total - high).astype(BF16)

    def hid_copy(j):
        there = hid.at[h, pl.ds(pl.multiple_of(c * SPAN, SPAN), SPAN), :]
        return remote(hid_send.at[j], there, hid_ss.at[j], hid_rs.at[arrives_as[j]], (s, planes[j]))

    def sum_copy(j):
        return remote(sums_send.at[j], sums.at[h, c], sum_ss.at[j], sum_rs.at[arrives_as[j]], (s, planes[j]))

    for j in (0, 1, 2):
        def put(lanes, value, j=j):
            hid_send[j, :, lanes] = value

        sums_send[j] = finish(planes[j], put)
        hid_copy(j).start()
        sum_copy(j).start()
        for k in range(4):
            step_copy(1, j, k).wait_recv()
            step_copy(2, j, k).start()

    def put_own(lanes, value):
        hid[h, pl.ds(pl.multiple_of(c * SPAN, SPAN), SPAN), lanes] = value

    sums[h, c] = finish(h, put_own)

    for j in (0, 1):
        for m in range(DIRECT_PIECES // 2, DIRECT_PIECES):
            direct_copy(j, m).start()

    def forward(n, plane):
        part = hid.at[plane, pl.ds(pl.multiple_of(c * SPAN, SPAN), SPAN), :]
        return remote(part, part, fwd_ss.at[n], fwd_rs.at[n], other)

    def forward_sums(n, plane):
        part = sums.at[plane, c]
        return remote(part, part, fsum_ss.at[n], fsum_rs.at[n], other)

    forward(3, h).start()
    forward_sums(3, h).start()

    for j in (0, 1, 2):
        for k in range(4):
            step_copy(2, j, k).wait_recv()
            step_copy(3, j, k).start()

    own_weight.wait()
    forward(3, h).wait_recv()

    @pl.loop(0, 8)
    def _(n):
        lanes = pl.ds(pl.multiple_of(n * 256, 256), 256)
        acc[:, lanes] = jnp.dot(hid[h], weight[h, :, lanes], preferred_element_type=F32)

    def wait_hid(j):
        part = hid.at[planes[j], pl.ds(pl.multiple_of(c * SPAN, SPAN), SPAN), :]
        remote(part, part, hid_ss.at[j], hid_rs.at[j], (s, planes[j])).wait_recv()
        tot = sums.at[planes[j], c]
        remote(tot, tot, sum_ss.at[j], sum_rs.at[j], (s, planes[j])).wait_recv()
        forward(j, planes[j]).start()
        forward_sums(j, planes[j]).start()

    def multiply(j, k, last):
        first = (mine[k] // 8) * 512
        if last:
            first = 512 - first
        depth = pl.ds(pl.multiple_of(first, 512), 512)
        lanes = slice(k * WIDTHS[j], (k + 1) * WIDTHS[j])
        acc[:, lanes] += jnp.dot(hid[planes[j], :, depth], weight[planes[j], depth, lanes], preferred_element_type=F32)

    for j in (0, 1, 2):
        wait_hid(j)
        forward(j, planes[j]).wait_recv()
        for k in range(4):
            multiply(j, k, False)
    for j in (0, 1):
        for m in range(DIRECT_PIECES):
            direct_wait(j, m)
        for n in range(DIRECT // 256):
            lanes = slice(2048 - DIRECT + n * 256, 2048 - DIRECT + (n + 1) * 256)
            acc[:, lanes] += jnp.dot(hid[planes[j]], weight[planes[j], :, lanes], preferred_element_type=F32)
    for j in (0, 1, 2):
        for k in range(4):
            step_copy(3, j, k).wait_recv()
            multiply(j, k, True)

    forward_sums(3, h).wait_recv()
    for j in (0, 1, 2):
        forward_sums(j, planes[j]).wait_recv()

    def scales(core):
        total = jnp.zeros((16, SPAN), F32)
        for n in range(4):
            total = total + sums[n, core].astype(F32)
        both = lax.rsqrt((total[0:1] + total[1:2]) / INNER + 1e-05)
        return jnp.broadcast_to(both, (128, SPAN)).T

    def finished(core, slot):
        factor = scales(core)
        factor = jnp.concatenate([factor, factor], axis=1)

        @pl.loop(0, 8)
        def _(n):
            lanes = pl.ds(pl.multiple_of(n * 256, 256), 256)
            rows = pl.ds(pl.multiple_of(core * SPAN, SPAN), SPAN)
            out_buf[slot, :, lanes] = (acc[rows, lanes] * factor).astype(BF16)

    columns = pl.ds(pl.multiple_of(base, 128), 2048)
    finished(1 - c, 0)
    send_out = remote(out_buf.at[0], out_hbm.at[:, columns], out_ss, out_rs, other)
    send_out.start()
    finished(c, 1)
    keep = pltpu.make_async_copy(out_buf.at[1], out_hbm.at[:, columns], out_sem)
    keep.start()

    for j in (0, 1, 2):
        for k in range(4):
            slice_copy(j, k).wait_send()
            for t in range(4):
                step_copy(t, j, k).wait_send()
        hid_copy(j).wait_send()
        sum_copy(j).wait_send()
        forward(j, planes[j]).wait_send()
        forward_sums(j, planes[j]).wait_send()
    for j in (0, 1):
        for m in range(DIRECT_PIECES):
            direct_copy(j, m).wait_send()
    forward(3, h).wait_send()
    forward_sums(3, h).wait_send()

    @pl.loop(1, 32)
    def _(i):
        chunk_copy(i).wait_send()
        inc_copy(i).wait_send()

    keep.wait()
    send_out.wait()


def local(xs, gate_branch, bmat, cmat, dt_code, resets, decay_rate, skip, norm_gain, out_weight):
    vmem = pl.BlockSpec(memory_space=pltpu.VMEM)
    hbm = pl.BlockSpec(memory_space=pl.ANY)
    smem = pl.BlockSpec(memory_space=pltpu.SMEM)
    dma = pltpu.SemaphoreType.DMA
    V = pltpu.VMEM
    return pl.pallas_call(
        kernel,
        out_shape=jax.ShapeDtypeStruct((256, 4096), BF16),
        in_specs=[hbm, hbm, vmem, vmem, vmem, vmem, vmem, hbm, smem, smem],
        out_specs=hbm,
        scratch_shapes=[
            V((1024, 1024), BF16),
            V((1024, 1024), BF16),
            V((4, 1024, 2048), BF16),
            V((4, 512, 1024), BF16),
            V((3, 256, 1024), BF16),
            V((4, 2, 16, 256), BF16),
            V((3, 16, 256), BF16),
            V((512, 2048), F32),
            V((2, 256, 2048), BF16),
            V((256, 256), BF16),
            V((4, 256, 128), F32),
            V((4, 256, 256), BF16),
            V((4, 128, 256), BF16),
            V((4, 16, 256), F32),
            V((4, 8, 256), F32),
            V((1024, 1024), F32),
            V((4, 8, 128, 128), F32),
            V((4, 8, 8, 128), F32),
            V((32, 48, 128), BF16),
            V((32, 48, 128), BF16),
            V((32, 32, 128), BF16),
            V((32, 32, 128), BF16),
            V((256, 256), F32),
            V((1024, 1024), F32),
            dma((2,)), dma, dma((3, 4)), dma((3, 4)),
            dma((2, DIRECT_PIECES)), dma((2, DIRECT_PIECES)), dma((4, 3, 4)), dma((4, 3, 4)),
            dma((32,)), dma((32,)), dma((32,)), dma((32,)),
            dma((3,)), dma((3,)), dma((3,)), dma((3,)), dma((4,)), dma((4,)), dma((4,)), dma((4,)),
            dma, dma, dma,
        ],
        compiler_params=pltpu.CompilerParams(
            collective_id=0, has_side_effects=True, vmem_limit_bytes=64 * 1024 * 1024 - 65536
        ),
    )(
        xs, gate_branch, bmat, cmat, dt_code, resets.reshape(1, 1024), norm_gain.reshape(1, 1024), out_weight,
        decay_rate, skip,
    )


def solution(mesh):
    in_specs = (
        P("seq", "head"),
        P("seq", "head"),
        P("seq", None),
        P("seq", None),
        P("head", "seq"),
        P("seq"),
        P("head"),
        P("head"),
        P("head"),
        P("head", None),
    )
    out_specs = P(("seq", "head"), None)
    return jax.shard_map(local, mesh=mesh, in_specs=in_specs, out_specs=out_specs, check_vma=False)
```

time: 222 us -> 92.8 us (0.42)
  waiting for transfers between devices: 115 us -> 0 us
  Pallas kernels: 0 us -> 89.5 us
  matrix products: 32.6 us -> 0 us
  local copies, waits for them, and re-layouts: 23.8 us -> 3.13 us
  other arithmetic: 18.8 us -> 0 us
  between operations: 13.7 us -> 0.01 us
  starting transfers between devices: 9.46 us -> 0 us
  blocking collectives: 8.02 us -> 0 us
    pallas_call x0 -> x1, Pallas kernels: none -> 89.5 us  [local(): pl.pallas_call(kernel, out_shape=jax.ShapeDtypeStruct((256, 4096), BF16),...]
    reduce_scatter x1 -> x0, waiting for transfers between devices: 79.3 us -> none  [local(): lax.psum_scatter(jnp.dot(hidden, out_weight, preferred_element_type=jnp.f...]
    all_gather x1 -> x0, waiting for transfers between devices: 35.9 us -> none  [local(): lax.all_gather(running[None].astype(jnp.bfloat16), 'seq', axis=0, tiled=T...]
    dot_general x6 -> x0, matrix products: 32.6 us -> none  [the longest x1 15.9 us: local(): jnp.dot(hidden, out_weight, preferred_element_type=jnp.float32)]
    convert_element_type x2 -> x0, local copies, waits for them, and re-layouts: 9.74 us -> none  [local(): scaled = (raw_values.astype(jnp.float32) * step_scale).astype(jnp.bfloat16)]
    all_to_all x1 -> x0, starting transfers between devices: 9.42 us -> none  [copy_for_each(): return lax.all_to_all(copies, axis, split_axis=0, concat_axis=0, tiled=True)]
    all_to_all x1 -> x0, blocking collectives: 8.02 us -> none  [copy_for_each(): return lax.all_to_all(copies, axis, split_axis=0, concat_axis=0, tiled=True)]
    convert_element_type x3 -> x0, other arithmetic: 6.56 us -> none  [the longest x1 4.92 us: local(): (scaled.astype(jnp.float32) * to_end.transpose(1, 2, 0)[:, :, :, None]).a...]
  transfers between devices with their start and end apart: 3 -> 0, of which waited for: 2 -> 0; matrix products, arithmetic and copies ran while one was open for 5% -> 0% of each run, Pallas kernels for 0% -> 0%
where the time goes in v1:
time: 92.8 us; the launch traced here: 92.6 us
  Pallas kernels  89.5 us (96%)
  local copies, waits for them, and re-layouts  3.13 us (3%)
    pallas_call x1, Pallas kernels, local(): pl.pallas_call(kernel, out_shape=jax.ShapeDtypeStruct((256, 4096), BF16),...  89.5 us
    unnamed x1, local copies, waits for them, and re-layouts  3.13 us

profile of v1, /device:TPU:1, one launch (start us, length us, event | category | flops | bytes accessed | tf_op | source)
XLA Modules:
  0.0 92.6 jit_solution(14433573223557404183)
XLA Ops:
  0.0 89.5 %shard_map.100 = bf16[256,4096]{1,0:T(8,128)(2,1)} custom-call(bf16[1024,1024]{1,0:T(8,128)(2,1)} %xs_hbm.1, bf16[1024,1024]{1,0:T(8,128)(2,1)} %gate_hbm.1, bf16[1024,128]{1,0:T(8,128)(2,1)} %bmat.1, bf16[1024,128]{1,0:T(8,128)(2,1)} %cmat.1, s32[16,1024]{1,0:T(8,128)} %dt.1, s32[1,1024]{1,0:T(1,128)} %bitcast.2, f32[1,1024]{1,0:T(1,128)} %bitcast.3, ...), custom_call_target="tpu_custom_call" | custom-call | tf_op jit(solution)/shard_map/pallas_call | solution.py:423
  89.5 3.1 %copy.12 = bf16[256,4096]{1,0:T(8,128)(2,1)} copy(bf16[256,4096]{1,0:T(8,128)(2,1)} %shard_map.100) | data formatting | bytes 4194304

commit v2 on v1

v2 whole, which is shorter than its diff:
```python
import jax
import jax.numpy as jnp
from jax import lax
from jax.experimental import pallas as pl
from jax.experimental.pallas import tpu as pltpu
from jax.sharding import PartitionSpec as P

HEAD_DIM = 64
STATE = 128
SPAN = 256
INNER = 4096
MESH = pl.DeviceIdType.MESH
LOG2E = 1.4426950408889634
F32 = jnp.float32
BF16 = jnp.bfloat16

WIDTHS = (384, 384, 512)
DIRECT = 512
DIRECT_PIECES = 2


def iota(shape, dim):
    return lax.broadcasted_iota(jnp.int32, shape, dim)


def kernel(
    xs_hbm, gate_hbm, bmat, cmat, dt, resets, gain, w_hbm, rate, skip,
    out,
    xs, gate, weight, hid, hid_send, sums, sums_send, acc, out_send,
    tri, col, split, bt, cjp, cntrow, grow, starts, reach, whole_send, pair_recv, chunk_send, chunk_recv, inc_send, inc_recv,
    pair_out, incoming, cbm, local,
    in_sem, own_sem, slice_ss, slice_rs, direct_ss, direct_rs, step_ss, step_rs,
    pair_ss, pair_rs, chunk_ss, chunk_rs, inc_ss, inc_rs, last_ss, last_rs, hid_ss, hid_rs, sum_ss, sum_rs, fwd_ss, fwd_rs, fsum_ss, fsum_rs,
    out_ss, out_rs,
):
    s = lax.axis_index("seq")
    h = lax.axis_index("head")
    x, z, c = s // 8, (s // 2) % 4, s % 2
    other = (s + 1 - 2 * c, h)

    def remote(src, dst, ss, rs, dev):
        return pltpu.make_async_remote_copy(
            src_ref=src, dst_ref=dst, send_sem=ss, recv_sem=rs, device_id=dev, device_id_type=MESH
        )

    copies_in = [
        pltpu.make_async_copy(xs_hbm, xs, in_sem.at[0]),
        pltpu.make_async_copy(gate_hbm, gate, in_sem.at[1]),
    ]
    for cp in copies_in:
        cp.start()

    barrier = pltpu.get_barrier_semaphore()
    chip = s // 2

    def same_core(i):
        return ((chip + i) % 16 * 2 + c, h)

    @pl.loop(1, 16)
    def _(i):
        pl.semaphore_signal(barrier, inc=1, device_id=same_core(i), device_id_type=MESH)

    pl.semaphore_signal(barrier, inc=1, device_id=other, device_id_type=MESH)
    for d in (1, 2, 3):
        pl.semaphore_signal(barrier, inc=1, device_id=(s, (h + d) % 4), device_id_type=MESH)

    planes = [(h + 1) % 4, (h + 3) % 4, (h + 2) % 4]
    arrives_as = (1, 0, 2)

    px, pz = x % 2, z % 2
    ax, az = x // 2, z // 2
    bx, bz = ((x + 1) // 2) % 2, ((z + 1) // 2) % 2
    x_a, z_a = x + 1 - 2 * px, z + 1 - 2 * pz
    x_b, z_b = (x + 3 + 2 * px) % 4, (z + 3 + 2 * pz) % 4

    def at(xx, zz):
        return ((xx * 4 + zz) * 2 + c, h)

    along = (at(x_a, z), at(x, z_a), at(x_b, z), at(x, z_b))
    bits = ((px, pz, ax, az), (pz, px, az, bx), (px, pz, bx, bz), (pz, px, bz, ax))
    mine = [b0 + 2 * b1 + 4 * b2 + 8 * b3 for b0, b1, b2, b3 in bits]
    base = c * 2048

    def slice_copy(j, k):
        rows = pl.ds(pl.multiple_of(mine[k] * 64, 64), 64)
        width = WIDTHS[arrives_as[j]]
        src = w_hbm.at[rows, pl.ds(pl.multiple_of(base + k * width, 128), width)]
        dst = weight.at[h, rows, pl.ds(k * width, width)]
        return remote(src, dst, slice_ss.at[j], slice_rs.at[arrives_as[j]], (s, planes[j]))

    def slice_all(j):
        part = weight.at[planes[j], pl.ds(0, 64), pl.ds(0, 4 * WIDTHS[j])]
        return remote(part, part, slice_ss.at[arrives_as[j]], slice_rs.at[j], (s, planes[j]))

    per = 1024 // DIRECT_PIECES

    def direct_copy(j, m):
        rows = pl.ds(m * per, per)
        src = w_hbm.at[rows, pl.ds(pl.multiple_of(base + 2048 - DIRECT, 128), DIRECT)]
        dst = weight.at[h, rows, pl.ds(2048 - DIRECT, DIRECT)]
        return remote(src, dst, direct_ss.at[j, m], direct_rs.at[1 - j, m], (s, planes[j]))

    def direct_wait(j, m):
        part = weight.at[planes[j], pl.ds(m * per, per), pl.ds(2048 - DIRECT, DIRECT)]
        remote(part, part, direct_ss.at[j, m], direct_rs.at[j, m], (s, planes[j])).wait_recv()

    def step_parts(t, j):
        return 2 if (t, j) == (3, 2) else 1

    def step_copy(t, j, k, n):
        size = (64 << t) // step_parts(t, j)
        first = (mine[k] // (1 << t)) * (64 << t) + n * size
        rows = pl.ds(pl.multiple_of(first, size), size)
        part = weight.at[planes[j], rows, pl.ds(k * WIDTHS[j], WIDTHS[j])]
        return remote(part, part, step_ss.at[t, j + n], step_rs.at[t, j + n], along[(k + t) % 4])

    def step_all(t, j, n=0):
        part = weight.at[planes[j], pl.ds(0, (64 << t) // step_parts(t, j)), pl.ds(0, 4 * WIDTHS[j])]
        return remote(part, part, step_ss.at[t, j + n], step_rs.at[t, j + n], other)

    def step_send(t, j):
        for n in range(step_parts(t, j)):
            for k in range(4):
                step_copy(t, j, k, n).start()

    def relay(t, j):
        if t == 0:
            slice_all(j).wait_recv()
        else:
            step_all(t - 1, j).wait_recv()
        step_send(t, j)

    own_weight = pltpu.make_async_copy(w_hbm.at[:, pl.ds(pl.multiple_of(base, 128), 2048)], weight.at[h], own_sem)
    own_weight.start()

    tri[...] = jnp.where(iota((SPAN, SPAN), 0) <= iota((SPAN, SPAN), 1), 1.0, 0.0).astype(BF16)
    head_row = iota((16, SPAN), 0)
    slope = jnp.zeros((16, SPAN), F32)
    for n in range(16):
        slope = jnp.where(head_row == n, rate[n] * (-LOG2E / 16.0), slope)
    for b in range(4):
        d = dt[:, b * SPAN:(b + 1) * SPAN]
        flags = jnp.broadcast_to(resets[:, b * SPAN:(b + 1) * SPAN], (16, SPAN))
        parts = [d & 0xFF, d & 0xFF00, d & 0x30000, flags]
        stack = jnp.concatenate([p.astype(F32) for p in parts], axis=0).astype(BF16)
        run = jnp.dot(stack, tri[...], preferred_element_type=F32)
        c2 = (run[0:16] + run[16:32] + run[32:48]) * slope
        count = run[48:64]
        ls = jnp.log(jnp.minimum(d.astype(F32) * 0.0625, 1.0)) * LOG2E
        c2_end, count_end = c2[:, SPAN - 1:SPAN], count[:, SPAN - 1:SPAN]
        from_start = jnp.where(count == 0, jnp.exp2(c2), 0.0)
        to_end = jnp.where(count == count_end, jnp.exp2(c2_end - c2 + ls), 0.0)
        cjp[b] = c2 - ls
        cntrow[b] = count[0:8]
        table = jnp.concatenate([c2, from_start, to_end, count, jnp.zeros((64, SPAN), F32)], axis=0)
        flipped = table.T
        col[b] = flipped
        high = flipped.astype(BF16)
        low = (flipped - high.astype(F32)).astype(BF16)
        split[b] = jnp.concatenate([high, low], axis=1)
        bt[b] = bmat[b * SPAN:(b + 1) * SPAN, :].T

    pl.semaphore_wait(barrier, 19)

    for j in (0, 1):
        for k in range(4):
            slice_copy(j, k).start()

    copies_in[0].wait()

    def in_parts(row):
        high = row.astype(BF16).astype(F32)
        mid = (row - high).astype(BF16).astype(F32)
        line = iota((16, 128), 0)
        low = row - high - mid
        return jnp.where(line == 0, high, jnp.where(line == 1, mid, jnp.where(line == 2, low, 0.0))).astype(BF16)

    def from_parts(rows):
        rows = rows.astype(F32)
        return rows[0:1] + rows[1:2] + rows[2:3]

    def states(group):
        row, lane = iota((SPAN, SPAN), 0) % 128, iota((SPAN, SPAN), 1)
        wides, fresh = {}, {}
        for q in group:
            pick = jnp.where(lane < 128, 16, 32) + 2 * q + (lane % 128) // 64
            pick = jnp.where(row == pick, 1.0, 0.0).astype(BF16)
            for b in range(4):
                wides[q, b] = jnp.dot(split[b], pick, preferred_element_type=F32)
        for q in group:
            lanes = slice(q * 128, (q + 1) * 128)
            for b in range(4):
                rows = slice(b * SPAN, (b + 1) * SPAN)
                grow[rows, lanes] = wides[q, b][:, 0:128]
                weighted = (xs[rows, lanes].astype(F32) * wides[q, b][:, 128:256]).astype(BF16)
                fresh[q, b] = jnp.dot(bt[b], weighted, preferred_element_type=F32)
        for q in group:
            run = jnp.zeros((STATE, 128), F32)
            product = jnp.ones((1, 128), F32)
            for b in range(4):
                starts[b, q] = run
                reach[b, q] = jnp.broadcast_to(product, (8, 128))
                through = wides[q, b][SPAN - 1:SPAN, 0:128]
                run = through * run + fresh[q, b]
                product = product * through
            whole_send[q, 0:128, :] = run.astype(BF16)
            whole_send[q, 128:144, :] = in_parts(product)

    for q in range(0, 8, 2):
        states((q, q + 1))

    theirs = whole_send.at[pl.ds(4 - 4 * c, 4)]
    pair = remote(theirs, pair_recv, pair_ss, pair_rs, other)
    pair.start()

    half = SPAN // 2

    def inside(b):
        rows = pl.ds(pl.multiple_of(b * SPAN, SPAN), SPAN)
        table = col[b]
        pair = jnp.dot(cmat[rows, :], bt[b], preferred_element_type=F32)
        same = (table[:, 48:49] == cntrow[b][0:1, :]) & (iota((SPAN, SPAN), 1) <= iota((SPAN, SPAN), 0))
        cbm[...] = jnp.where(same, pair, 0.0)
        first = iota((SPAN, 128), 1) < HEAD_DIM
        for q in range(8):
            lanes = slice(q * 128, (q + 1) * 128)
            value = xs[rows, lanes]
            value_float = value.astype(F32)
            sides = (jnp.where(first, value_float, 0.0).astype(BF16), jnp.where(first, 0.0, value_float).astype(BF16))
            total = [jnp.where(first[0:half], skip[2 * q], skip[2 * q + 1]) * value_float[r * half:(r + 1) * half] for r in (0, 1)]
            for e in (0, 1):
                n = 2 * q + e
                ci = table[:, n:n + 1]
                cj = cjp[b, n:n + 1, :]
                for r in (0, 1):
                    lo, hi = r * half, (r + 1) * half
                    gap = jnp.minimum(ci[lo:hi] - cj[:, 0:hi], 0.0)
                    score = (jnp.exp2(gap) * cbm[lo:hi, 0:hi]).astype(BF16)
                    total[r] = total[r] + jnp.dot(score, sides[e][0:hi], preferred_element_type=F32)
            for r in (0, 1):
                local[pl.ds(pl.multiple_of(b * SPAN + r * half, half), half), lanes] = total[r]

    inside(0)

    pair.wait_recv()
    first_core = c == 0
    for n in range(4):
        own, far = whole_send[4 * c + n], pair_recv[n]
        own_through, far_through = from_parts(own[128:144]), from_parts(far[128:144])
        own_state, far_state = own[0:128].astype(F32), far[0:128].astype(F32)
        earlier = jnp.where(first_core, own_state, far_state)
        later = jnp.where(first_core, far_state, own_state)
        total = jnp.where(first_core, far_through, own_through) * earlier + later
        tail = in_parts(own_through * far_through)
        for r in range(4):
            chunk_send[n * 4 + r, 0:32, :] = total[r * 32:(r + 1) * 32].astype(BF16)
            chunk_send[n * 4 + r, 32:48, :] = tail

    @pl.loop(1, 16)
    def _(i):
        remote(chunk_send.at[(chip + i) % 16], chunk_recv.at[chip], chunk_ss, chunk_rs, same_core(i)).start()

    chunk_recv[chip] = chunk_send[chip]

    for k in range(4):
        slice_copy(2, k).start()
    inside(1)
    inside(2)
    for j in (0, 1):
        direct_copy(j, 0).start()

    relay(0, 0)
    relay(0, 1)

    arrived = chunk_recv.at[pl.ds(0, 15)]
    chunk_all = remote(arrived, arrived, chunk_ss, chunk_rs, other)
    chunk_all.wait_recv()

    state = jnp.zeros((32, 128), F32)
    for t in range(16):
        inc_send[t] = state.astype(BF16)
        state = from_parts(chunk_recv[t, 32:48, :]) * state + chunk_recv[t, 0:32, :].astype(F32)

    @pl.loop(1, 16)
    def _(i):
        remote(inc_send.at[(chip + i) % 16], inc_recv.at[chip], inc_ss, inc_rs, same_core(i)).start()

    inc_recv[chip] = inc_send[chip]

    inside(3)
    relay(1, 0)
    relay(1, 1)
    relay(0, 2)

    returned = inc_recv.at[pl.ds(0, 15)]
    inc_all = remote(returned, returned, inc_ss, inc_rs, other)
    inc_all.wait_recv()
    for n in range(4):
        own, far = whole_send[4 * c + n], pair_recv[n]
        first_state = jnp.where(first_core, own[0:128].astype(F32), far[0:128].astype(F32))
        first_through = jnp.where(first_core, from_parts(own[128:144]), from_parts(far[128:144]))
        reaching = inc_recv[n * 4:(n + 1) * 4].reshape(STATE, 128)
        second = (first_through * reaching.astype(F32) + first_state).astype(BF16)
        incoming[4 * c + n] = jnp.where(first_core, reaching.astype(F32), second.astype(F32)).astype(BF16)
        pair_out[n] = jnp.where(first_core, second.astype(F32), reaching.astype(F32)).astype(BF16)
    handed = remote(pair_out, incoming.at[pl.ds(4 * c, 4)], last_ss, last_rs, other)
    handed.start()
    relay(2, 0)
    relay(2, 1)
    handed.wait_recv()
    copies_in[1].wait()

    def finish(b, put):
        rows = pl.ds(pl.multiple_of(b * SPAN, SPAN), SPAN)
        query = cmat[rows, :]

        def part(q, squares):
            lanes = pl.ds(pl.multiple_of(q * 128, 128), 128)
            state = (starts[b, q] + reach[b, q, 0:1, :] * incoming[q].astype(F32)).astype(BF16)
            inter = jnp.dot(query, state, preferred_element_type=F32)
            value = local[rows, lanes] + grow[rows, lanes] * inter
            v = gate[rows, lanes].astype(F32)
            gated = value * (v / (1.0 + jnp.exp(-v)))
            put(lanes, (gated * gain[:, lanes]).astype(BF16))
            return squares + gated * gated

        squares = lax.fori_loop(0, 8, part, jnp.zeros((SPAN, 128), F32))
        total = jnp.broadcast_to(jnp.sum(squares, axis=1, keepdims=True), (SPAN, 128)).T[0:16, :]
        high = total.astype(BF16).astype(F32)
        return jnp.where(iota((16, SPAN), 0) == 0, high, total - high).astype(BF16)

    def hid_copy(j):
        there = hid.at[h, pl.ds(pl.multiple_of(c * SPAN, SPAN), SPAN), :]
        return remote(hid_send.at[j], there, hid_ss.at[j], hid_rs.at[arrives_as[j]], (s, planes[j]))

    def sum_copy(j):
        return remote(sums_send.at[j], sums.at[c, h], sum_ss, sum_rs, (s, planes[j]))

    for j in (0, 1, 2):
        def put(lanes, value, j=j):
            hid_send[j, :, lanes] = value

        sums_send[j] = finish(planes[j], put)
        hid_copy(j).start()
        sum_copy(j).start()
        if j == 0:
            relay(1, 2)

    def put_own(lanes, value):
        hid[h, pl.ds(pl.multiple_of(c * SPAN, SPAN), SPAN), lanes] = value

    sums[c, h] = finish(h, put_own)

    for j in (0, 1):
        direct_copy(j, 1).start()

    def forward(n, plane):
        part = hid.at[plane, pl.ds(pl.multiple_of(c * SPAN, SPAN), SPAN), :]
        return remote(part, part, fwd_ss.at[n], fwd_rs.at[n], other)

    forward(3, h).start()

    relay(3, 0)
    relay(2, 2)
    relay(3, 1)

    own_weight.wait()
    forward(3, h).wait_recv()

    @pl.loop(0, 8)
    def _(n):
        lanes = pl.ds(pl.multiple_of(n * 256, 256), 256)
        acc[:, lanes] = jnp.dot(hid[h], weight[h, :, lanes], preferred_element_type=F32)

    relay(3, 2)

    def wait_hid(j):
        part = hid.at[planes[j], pl.ds(pl.multiple_of(c * SPAN, SPAN), SPAN), :]
        remote(part, part, hid_ss.at[j], hid_rs.at[j], (s, planes[j])).wait_recv()
        forward(j, planes[j]).start()

    def depth_of(k, last, n, parts):
        first = (mine[k] // 8) * 512
        if last:
            first = 512 - first
        size = 512 // parts
        return pl.ds(pl.multiple_of(first + n * size, size), size)

    def multiply(j, k, last, n=0, parts=1):
        depth = depth_of(k, last, n, parts)
        lanes = slice(k * WIDTHS[j], (k + 1) * WIDTHS[j])
        acc[:, lanes] += jnp.dot(hid[planes[j], :, depth], weight[planes[j], depth, lanes], preferred_element_type=F32)

    for j in (0, 1, 2):
        wait_hid(j)
    totals = sums.at[c, pl.ds(0, 3)]
    remote(totals, totals, sum_ss, sum_rs, other).wait_recv()
    forward_sums = remote(sums.at[c], sums.at[c], fsum_ss, fsum_rs, other)
    forward_sums.start()
    for j in (0, 1, 2):
        forward(j, planes[j]).wait_recv()
        for k in range(4):
            multiply(j, k, False)

    forward_sums.wait_recv()

    def scales(core):
        total = jnp.zeros((16, SPAN), F32)
        for n in range(4):
            total = total + sums[core, n].astype(F32)
        both = lax.rsqrt((total[0:1] + total[1:2]) / INNER + 1e-05)
        return jnp.broadcast_to(both, (128, SPAN)).T

    factors = [scales(core) for core in (1 - c, c)]

    for j in (0, 1):
        for m in range(DIRECT_PIECES):
            direct_wait(j, m)
        for n in range(DIRECT // 256):
            lanes = slice(2048 - DIRECT + n * 256, 2048 - DIRECT + (n + 1) * 256)
            acc[:, lanes] += jnp.dot(hid[planes[j]], weight[planes[j], :, lanes], preferred_element_type=F32)
    for j in (0, 1):
        step_all(3, j).wait_recv()
        for k in range(4):
            multiply(j, k, True)
    step_all(3, 2, 0).wait_recv()
    for k in range(4):
        multiply(2, k, True, 0, 2)
    step_all(3, 2, 1).wait_recv()

    out_copies = []
    for turn, core in enumerate((1 - c, c)):
        rows = pl.ds(pl.multiple_of(core * SPAN, SPAN), SPAN)
        factor = jnp.concatenate([factors[turn]] * 4, axis=1)
        for k in range(4):
            depth = depth_of(k, True, 1, 2)
            lanes = slice(k * 512, (k + 1) * 512)
            columns = pl.ds(pl.multiple_of(c * 2048 + k * 512, 512), 512)
            last = jnp.dot(hid[planes[2], rows, depth], weight[planes[2], depth, lanes], preferred_element_type=F32)
            value = ((acc[rows, lanes] + last) * factor).astype(BF16)
            if turn == 0:
                out_send[:, lanes] = value
                copy = remote(out_send.at[:, lanes], out.at[:, columns], out_ss, out_rs, other)
                copy.start()
            else:
                out[:, columns] = value

    for j in (0, 1, 2):
        slice_all(j).wait_send()
        for t in range(4):
            for n in range(step_parts(t, j)):
                step_all(t, j, n).wait_send()
        hid_copy(j).wait_send()
        forward(j, planes[j]).wait_send()
    totals_sent = remote(sums_send, sums_send, sum_ss, sum_rs, other)
    totals_sent.wait_send()
    for j in (0, 1):
        for m in range(DIRECT_PIECES):
            direct_copy(j, m).wait_send()
    forward(3, h).wait_send()
    forward_sums.wait_send()
    pair.wait_send()
    chunk_all.wait_send()
    inc_all.wait_send()
    handed.wait_send()
    whole = remote(out_send, out_send, out_ss, out_rs, other)
    whole.wait_send()
    whole.wait_recv()


def local(xs, gate_branch, bmat, cmat, dt_code, resets, decay_rate, skip, norm_gain, out_weight):
    vmem = pl.BlockSpec(memory_space=pltpu.VMEM)
    hbm = pl.BlockSpec(memory_space=pl.ANY)
    smem = pl.BlockSpec(memory_space=pltpu.SMEM)
    dma = pltpu.SemaphoreType.DMA
    V = pltpu.VMEM
    return pl.pallas_call(
        kernel,
        out_shape=pltpu.VMEM((256, 4096), BF16),
        in_specs=[hbm, hbm, vmem, vmem, vmem, vmem, vmem, hbm, smem, smem],
        out_specs=vmem,
        scratch_shapes=[
            V((1024, 1024), BF16),
            V((1024, 1024), BF16),
            V((4, 1024, 2048), BF16),
            V((4, 512, 1024), BF16),
            V((3, 256, 1024), BF16),
            V((2, 4, 16, 256), BF16),
            V((3, 16, 256), BF16),
            V((512, 2048), F32),
            V((256, 2048), BF16),
            V((256, 256), BF16),
            V((4, 256, 128), F32),
            V((4, 256, 256), BF16),
            V((4, 128, 256), BF16),
            V((4, 16, 256), F32),
            V((4, 8, 256), F32),
            V((1024, 1024), F32),
            V((4, 8, 128, 128), F32),
            V((4, 8, 8, 128), F32),
            V((8, 144, 128), BF16),
            V((4, 144, 128), BF16),
            V((16, 48, 128), BF16),
            V((16, 48, 128), BF16),
            V((16, 32, 128), BF16),
            V((16, 32, 128), BF16),
            V((4, 128, 128), BF16),
            V((8, 128, 128), BF16),
            V((256, 256), F32),
            V((1024, 1024), F32),
            dma((2,)), dma, dma((3,)), dma((3,)),
            dma((2, DIRECT_PIECES)), dma((2, DIRECT_PIECES)), dma((4, 4)), dma((4, 4)),
            dma, dma, dma, dma, dma, dma, dma, dma,
            dma((3,)), dma((3,)), dma, dma, dma((4,)), dma((4,)), dma, dma,
            dma, dma,
        ],
        compiler_params=pltpu.CompilerParams(
            collective_id=0, has_side_effects=True, vmem_limit_bytes=58 * 1024 * 1024
        ),
    )(
        xs, gate_branch, bmat, cmat, dt_code, resets.reshape(1, 1024), norm_gain.reshape(1, 1024), out_weight,
        decay_rate, skip,
    )


def solution(mesh):
    in_specs = (
        P("seq", "head"),
        P("seq", "head"),
        P("seq", None),
        P("seq", None),
        P("head", "seq"),
        P("seq"),
        P("head"),
        P("head"),
        P("head"),
        P("head", None),
    )
    out_specs = P(("seq", "head"), None)
    return jax.shard_map(local, mesh=mesh, in_specs=in_specs, out_specs=out_specs, check_vma=False)
```

time: 92.8 us -> 77.8 us (0.84)
  Pallas kernels: 89.5 us -> 76.3 us
  local copies, waits for them, and re-layouts: 3.13 us -> 1.32 us
    pallas_call x1, Pallas kernels: 89.5 us -> 76.3 us  [local(): pl.pallas_call(kernel, out_shape=pltpu.VMEM((256, 4096), BF16), in_specs=...]
    unnamed x1, local copies, waits for them, and re-layouts: 3.13 us -> 1.32 us
where the time goes in v2:
time: 77.8 us; the launch traced here: 77.7 us
  Pallas kernels  76.3 us (98%)
  local copies, waits for them, and re-layouts  1.32 us (2%)
    pallas_call x1, Pallas kernels, local(): pl.pallas_call(kernel, out_shape=pltpu.VMEM((256, 4096), BF16), in_specs=...  76.3 us

profile of v2, /device:TPU:1, one launch (start us, length us, event | category | flops | bytes accessed | tf_op | source)
XLA Modules:
  0.0 77.7 jit_solution(13915315654795805816)
XLA Ops:
  0.0 76.3 %shard_map.100 = bf16[256,4096]{1,0:T(8,128)(2,1)S(1)} custom-call(bf16[1024,1024]{1,0:T(8,128)(2,1)} %xs_hbm.1, bf16[1024,1024]{1,0:T(8,128)(2,1)} %gate_hbm.1, bf16[1024,128]{1,0:T(8,128)(2,1)} %bmat.1, bf16[1024,128]{1,0:T(8,128)(2,1)} %cmat.1, s32[16,1024]{1,0:T(8,128)} %dt.1, s32[1,1024]{1,0:T(1,128)} %bitcast.2, f32[1,1024]{1,0:T(1,128)} %bitcast.3, ...), custom_call_target="tpu_custom_call" | custom-call | tf_op jit(solution)/shard_map/pallas_call | solution.py:477
  76.3 1.3 %copy.12 = bf16[256,4096]{1,0:T(8,128)(2,1)} copy(bf16[256,4096]{1,0:T(8,128)(2,1)S(1)} %shard_map.100) | data formatting | bytes 4194304

commit v3 on v2

--- a/solution.py
+++ b/solution.py
@@ -14,9 +14,15 @@
 F32 = jnp.float32
 BF16 = jnp.bfloat16
 
-WIDTHS = (384, 384, 512)
-DIRECT = 512
+COLOURS = (
+    ((0, 384), (384, 256), (640, 384), (1024, 256)),
+    ((0, 256), (256, 384), (640, 256), (896, 384)),
+    ((0, 512), (512, 512), (1024, 512), (1536, 512)),
+)
+DIRECT = slice(1280, 1536)
 DIRECT_PIECES = 2
+PRODUCT = slice(1536, 2048)
+LAST = ((0, 256), (256, 128), (384, 128))
 
 
 def iota(shape, dim):
@@ -24,12 +30,12 @@
 
 
 def kernel(
-    xs_hbm, gate_hbm, bmat, cmat, dt, resets, gain, w_hbm, rate, skip,
+    xs_hbm, gate_hbm, bmat_hbm, cmat_hbm, dt_hbm, resets_hbm, gain_hbm, w_hbm, rate, skip,
     out,
-    xs, gate, weight, hid, hid_send, sums, sums_send, acc, out_send,
+    xs, gate, bmat, cmat, dt, resets, gain, weight, hid, hid_send, hid_far, product_send, product_recv, sums, sums_send, acc, done,
     tri, col, split, bt, cjp, cntrow, grow, starts, reach, whole_send, pair_recv, chunk_send, chunk_recv, inc_send, inc_recv,
     pair_out, incoming, cbm, local,
-    in_sem, own_sem, slice_ss, slice_rs, direct_ss, direct_rs, step_ss, step_rs,
+    in_sem, own_sem, slice_ss, slice_rs, direct_ss, direct_rs, far_ss, far_rs, product_ss, product_rs, step_ss, step_rs,
     pair_ss, pair_rs, chunk_ss, chunk_rs, inc_ss, inc_rs, last_ss, last_rs, hid_ss, hid_rs, sum_ss, sum_rs, fwd_ss, fwd_rs, fsum_ss, fsum_rs,
     out_ss, out_rs,
 ):
@@ -43,13 +49,6 @@
             src_ref=src, dst_ref=dst, send_sem=ss, recv_sem=rs, device_id=dev, device_id_type=MESH
         )
 
-    copies_in = [
-        pltpu.make_async_copy(xs_hbm, xs, in_sem.at[0]),
-        pltpu.make_async_copy(gate_hbm, gate, in_sem.at[1]),
-    ]
-    for cp in copies_in:
-        cp.start()
-
     barrier = pltpu.get_barrier_semaphore()
     chip = s // 2
 
@@ -63,6 +62,12 @@
     pl.semaphore_signal(barrier, inc=1, device_id=other, device_id_type=MESH)
     for d in (1, 2, 3):
         pl.semaphore_signal(barrier, inc=1, device_id=(s, (h + d) % 4), device_id_type=MESH)
+
+    sources = (dt_hbm, resets_hbm, bmat_hbm, cmat_hbm, xs_hbm, gate_hbm, gain_hbm)
+    places = (dt, resets, bmat, cmat, xs, gate, gain)
+    copies_in = [pltpu.make_async_copy(a, b, in_sem.at[n]) for n, (a, b) in enumerate(zip(sources, places))]
+    for cp in copies_in:
+        cp.start()
 
     planes = [(h + 1) % 4, (h + 3) % 4, (h + 2) % 4]
     arrives_as = (1, 0, 2)
@@ -81,47 +86,52 @@
     mine = [b0 + 2 * b1 + 4 * b2 + 8 * b3 for b0, b1, b2, b3 in bits]
     base = c * 2048
 
-    def slice_copy(j, k):
-        rows = pl.ds(pl.multiple_of(mine[k] * 64, 64), 64)
-        width = WIDTHS[arrives_as[j]]
-        src = w_hbm.at[rows, pl.ds(pl.multiple_of(base + k * width, 128), width)]
-        dst = weight.at[h, rows, pl.ds(k * width, width)]
-        return remote(src, dst, slice_ss.at[j], slice_rs.at[arrives_as[j]], (s, planes[j]))
+    def slice_send(j):
+        for k in range(4):
+            first, width = COLOURS[arrives_as[j]][k]
+            rows = pl.ds(pl.multiple_of(mine[k] * 64, 64), 64)
+            src = w_hbm.at[rows, pl.ds(pl.multiple_of(base + first, 128), width)]
+            dst = weight.at[h, rows, pl.ds(first, width)]
+            remote(src, dst, slice_ss.at[j], slice_rs.at[arrives_as[j]], (s, planes[j])).start()
+
+    def amount(t, j):
+        return weight.at[planes[j], pl.ds(0, 64 << t), pl.ds(0, 2048 if j == 2 else 1280)]
 
     def slice_all(j):
-        part = weight.at[planes[j], pl.ds(0, 64), pl.ds(0, 4 * WIDTHS[j])]
+        part = amount(0, j)
         return remote(part, part, slice_ss.at[arrives_as[j]], slice_rs.at[j], (s, planes[j]))
 
     per = 1024 // DIRECT_PIECES
 
     def direct_copy(j, m):
         rows = pl.ds(m * per, per)
-        src = w_hbm.at[rows, pl.ds(pl.multiple_of(base + 2048 - DIRECT, 128), DIRECT)]
-        dst = weight.at[h, rows, pl.ds(2048 - DIRECT, DIRECT)]
+        src = w_hbm.at[rows, pl.ds(pl.multiple_of(base + 1280, 128), 256)]
+        dst = weight.at[h, rows, pl.ds(1280, 256)]
         return remote(src, dst, direct_ss.at[j, m], direct_rs.at[1 - j, m], (s, planes[j]))
 
     def direct_wait(j, m):
-        part = weight.at[planes[j], pl.ds(m * per, per), pl.ds(2048 - DIRECT, DIRECT)]
+        part = weight.at[planes[j], pl.ds(m * per, per), pl.ds(1280, 256)]
         remote(part, part, direct_ss.at[j, m], direct_rs.at[j, m], (s, planes[j])).wait_recv()
 
     def step_parts(t, j):
-        return 2 if (t, j) == (3, 2) else 1
-
-    def step_copy(t, j, k, n):
-        size = (64 << t) // step_parts(t, j)
-        first = (mine[k] // (1 << t)) * (64 << t) + n * size
-        rows = pl.ds(pl.multiple_of(first, size), size)
-        part = weight.at[planes[j], rows, pl.ds(k * WIDTHS[j], WIDTHS[j])]
-        return remote(part, part, step_ss.at[t, j + n], step_rs.at[t, j + n], along[(k + t) % 4])
+        return len(LAST) if (t, j) == (3, 2) else 1
 
     def step_all(t, j, n=0):
-        part = weight.at[planes[j], pl.ds(0, (64 << t) // step_parts(t, j)), pl.ds(0, 4 * WIDTHS[j])]
+        part = amount(t, j)
+        if (t, j) == (3, 2):
+            part = weight.at[planes[j], pl.ds(0, 512), pl.ds(0, 4 * LAST[n][1])]
         return remote(part, part, step_ss.at[t, j + n], step_rs.at[t, j + n], other)
 
     def step_send(t, j):
         for n in range(step_parts(t, j)):
             for k in range(4):
-                step_copy(t, j, k, n).start()
+                column, width = COLOURS[j][k]
+                if (t, j) == (3, 2):
+                    column, width = column + LAST[n][0], LAST[n][1]
+                first = (mine[k] // (1 << t)) * (64 << t)
+                rows = pl.ds(pl.multiple_of(first, 64 << t), 64 << t)
+                part = weight.at[planes[j], rows, pl.ds(column, width)]
+                remote(part, part, step_ss.at[t, j + n], step_rs.at[t, j + n], along[(k + t) % 4]).start()
 
     def relay(t, j):
         if t == 0:
@@ -133,7 +143,14 @@
     own_weight = pltpu.make_async_copy(w_hbm.at[:, pl.ds(pl.multiple_of(base, 128), 2048)], weight.at[h], own_sem)
     own_weight.start()
 
+    pl.semaphore_wait(barrier, 19)
+
+    slice_send(0)
+    slice_send(1)
+
     tri[...] = jnp.where(iota((SPAN, SPAN), 0) <= iota((SPAN, SPAN), 1), 1.0, 0.0).astype(BF16)
+    for n in (0, 1, 2):
+        copies_in[n].wait()
     head_row = iota((16, SPAN), 0)
     slope = jnp.zeros((16, SPAN), F32)
     for n in range(16):
@@ -160,13 +177,8 @@
         split[b] = jnp.concatenate([high, low], axis=1)
         bt[b] = bmat[b * SPAN:(b + 1) * SPAN, :].T
 
-    pl.semaphore_wait(barrier, 19)
-
-    for j in (0, 1):
-        for k in range(4):
-            slice_copy(j, k).start()
-
-    copies_in[0].wait()
+    copies_in[3].wait()
+    copies_in[4].wait()
 
     def in_parts(row):
         high = row.astype(BF16).astype(F32)
@@ -262,12 +274,12 @@
 
     chunk_recv[chip] = chunk_send[chip]
 
-    for k in range(4):
-        slice_copy(2, k).start()
+    slice_send(2)
     inside(1)
     inside(2)
-    for j in (0, 1):
-        direct_copy(j, 0).start()
+    for m in range(DIRECT_PIECES):
+        for j in (0, 1):
+            direct_copy(j, m).start()
 
     relay(0, 0)
     relay(0, 1)
@@ -287,9 +299,9 @@
 
     inc_recv[chip] = inc_send[chip]
 
-    inside(3)
     relay(1, 0)
     relay(1, 1)
+    inside(3)
     relay(0, 2)
 
     returned = inc_recv.at[pl.ds(0, 15)]
@@ -308,7 +320,8 @@
     relay(2, 0)
     relay(2, 1)
     handed.wait_recv()
-    copies_in[1].wait()
+    copies_in[5].wait()
+    copies_in[6].wait()
 
     def finish(b, put):
         rows = pl.ds(pl.multiple_of(b * SPAN, SPAN), SPAN)
@@ -333,26 +346,41 @@
         there = hid.at[h, pl.ds(pl.multiple_of(c * SPAN, SPAN), SPAN), :]
         return remote(hid_send.at[j], there, hid_ss.at[j], hid_rs.at[arrives_as[j]], (s, planes[j]))
 
+    def far_copy(j):
+        return remote(hid_send.at[j], hid_far.at[j], far_ss.at[j], far_rs.at[j], other)
+
+    def product_copy(j):
+        there = product_recv.at[arrives_as[j]]
+        return remote(product_send.at[j], there, product_ss.at[j], product_rs.at[arrives_as[j]], (s, planes[j]))
+
+    def product_all(j):
+        part = product_recv.at[j]
+        return remote(part, part, product_ss.at[j], product_rs.at[j], (s, planes[j]))
+
+
+    there, here = (pl.ds(pl.multiple_of(core * SPAN, SPAN), SPAN) for core in (1 - c, c))
+
     def sum_copy(j):
         return remote(sums_send.at[j], sums.at[c, h], sum_ss, sum_rs, (s, planes[j]))
 
-    for j in (0, 1, 2):
+    for j in (2, 0, 1):
         def put(lanes, value, j=j):
             hid_send[j, :, lanes] = value
 
         sums_send[j] = finish(planes[j], put)
         hid_copy(j).start()
         sum_copy(j).start()
-        if j == 0:
+        if j < 2:
+            far_copy(j).start()
+        if j == 2:
             relay(1, 2)
+
+    relay(3, 0)
 
     def put_own(lanes, value):
         hid[h, pl.ds(pl.multiple_of(c * SPAN, SPAN), SPAN), lanes] = value
 
     sums[c, h] = finish(h, put_own)
-
-    for j in (0, 1):
-        direct_copy(j, 1).start()
 
     def forward(n, plane):
         part = hid.at[plane, pl.ds(pl.multiple_of(c * SPAN, SPAN), SPAN), :]
@@ -360,11 +388,16 @@
 
     forward(3, h).start()
 
-    relay(3, 0)
+    own_weight.wait()
+    for j in (0, 1):
+        far_copy(j).wait_recv()
+        for rows, value in ((here, hid_send), (there, hid_far)):
+            product_send[j, rows, :] = jnp.dot(value[j], weight[h, :, PRODUCT], preferred_element_type=F32).astype(BF16)
+        product_copy(j).start()
+
     relay(2, 2)
     relay(3, 1)
 
-    own_weight.wait()
     forward(3, h).wait_recv()
 
     @pl.loop(0, 8)
@@ -372,35 +405,37 @@
         lanes = pl.ds(pl.multiple_of(n * 256, 256), 256)
         acc[:, lanes] = jnp.dot(hid[h], weight[h, :, lanes], preferred_element_type=F32)
 
-    relay(3, 2)
-
     def wait_hid(j):
         part = hid.at[planes[j], pl.ds(pl.multiple_of(c * SPAN, SPAN), SPAN), :]
         remote(part, part, hid_ss.at[j], hid_rs.at[j], (s, planes[j])).wait_recv()
         forward(j, planes[j]).start()
 
-    def depth_of(k, last, n, parts):
+    def depth_of(k, last):
         first = (mine[k] // 8) * 512
         if last:
             first = 512 - first
-        size = 512 // parts
-        return pl.ds(pl.multiple_of(first + n * size, size), size)
-
-    def multiply(j, k, last, n=0, parts=1):
-        depth = depth_of(k, last, n, parts)
-        lanes = slice(k * WIDTHS[j], (k + 1) * WIDTHS[j])
-        acc[:, lanes] += jnp.dot(hid[planes[j], :, depth], weight[planes[j], depth, lanes], preferred_element_type=F32)
-
-    for j in (0, 1, 2):
+        return pl.ds(pl.multiple_of(first, 512), 512)
+
+    def multiply(j, last):
+        for k in range(4):
+            depth = depth_of(k, last)
+            column, width = COLOURS[j][k]
+            lanes = slice(column, column + width)
+            acc[:, lanes] += jnp.dot(hid[planes[j], :, depth], weight[planes[j], depth, lanes], preferred_element_type=F32)
+
+    wait_hid(2)
+    forward(2, planes[2]).wait_recv()
+    relay(3, 2)
+    multiply(2, False)
+    for j in (0, 1):
         wait_hid(j)
     totals = sums.at[c, pl.ds(0, 3)]
     remote(totals, totals, sum_ss, sum_rs, other).wait_recv()
     forward_sums = remote(sums.at[c], sums.at[c], fsum_ss, fsum_rs, other)
     forward_sums.start()
-    for j in (0, 1, 2):
+    for j in (0, 1):
         forward(j, planes[j]).wait_recv()
-        for k in range(4):
-            multiply(j, k, False)
+        multiply(j, False)
 
     forward_sums.wait_recv()
 
@@ -411,39 +446,38 @@
         both = lax.rsqrt((total[0:1] + total[1:2]) / INNER + 1e-05)
         return jnp.broadcast_to(both, (128, SPAN)).T
 
-    factors = [scales(core) for core in (1 - c, c)]
-
+    scale_there, scale_here = scales(1 - c), scales(c)
+
+    for j in (0, 1):
+        step_all(3, j).wait_recv()
+        multiply(j, True)
     for j in (0, 1):
         for m in range(DIRECT_PIECES):
             direct_wait(j, m)
-        for n in range(DIRECT // 256):
-            lanes = slice(2048 - DIRECT + n * 256, 2048 - DIRECT + (n + 1) * 256)
-            acc[:, lanes] += jnp.dot(hid[planes[j]], weight[planes[j], :, lanes], preferred_element_type=F32)
-    for j in (0, 1):
-        step_all(3, j).wait_recv()
+        acc[:, DIRECT] += jnp.dot(hid[planes[j]], weight[planes[j], :, DIRECT], preferred_element_type=F32)
+    for j in (0, 1):
+        product_all(j).wait_recv()
+    acc[:, PRODUCT] += product_recv[0].astype(F32) + product_recv[1].astype(F32)
+
+    for n, (offset, width) in enumerate(LAST):
+        step_all(3, 2, n).wait_recv()
+        spans = [slice(k * 512 + offset, k * 512 + offset + width) for k in range(4)]
+        columns = [pl.ds(pl.multiple_of(base + k * 512 + offset, 128), width) for k in range(4)]
+
+        def ended(rows, scale):
+            scale = jnp.concatenate([scale] * (width // 128), axis=1)
+            terms = []
+            for k in range(4):
+                depth = depth_of(k, True)
+                terms.append(jnp.dot(hid[planes[2], rows, depth], weight[planes[2], depth, spans[k]], preferred_element_type=F32))
+            return [((acc[rows, spans[k]] + terms[k]) * scale).astype(BF16) for k in range(4)]
+
+        for k, value in enumerate(ended(there, scale_there)):
+            done[:, spans[k]] = value
         for k in range(4):
-            multiply(j, k, True)
-    step_all(3, 2, 0).wait_recv()
-    for k in range(4):
-        multiply(2, k, True, 0, 2)
-    step_all(3, 2, 1).wait_recv()
-
-    out_copies = []
-    for turn, core in enumerate((1 - c, c)):
-        rows = pl.ds(pl.multiple_of(core * SPAN, SPAN), SPAN)
-        factor = jnp.concatenate([factors[turn]] * 4, axis=1)
-        for k in range(4):
-            depth = depth_of(k, True, 1, 2)
-            lanes = slice(k * 512, (k + 1) * 512)
-            columns = pl.ds(pl.multiple_of(c * 2048 + k * 512, 512), 512)
-            last = jnp.dot(hid[planes[2], rows, depth], weight[planes[2], depth, lanes], preferred_element_type=F32)
-            value = ((acc[rows, lanes] + last) * factor).astype(BF16)
-            if turn == 0:
-                out_send[:, lanes] = value
-                copy = remote(out_send.at[:, lanes], out.at[:, columns], out_ss, out_rs, other)
-                copy.start()
-            else:
-                out[:, columns] = value
+            remote(done.at[:, spans[k]], out.at[:, columns[k]], out_ss, out_rs, other).start()
+        for k, value in enumerate(ended(here, scale_here)):
+            out[:, columns[k]] = value
 
     for j in (0, 1, 2):
         slice_all(j).wait_send()
@@ -455,6 +489,8 @@
     totals_sent = remote(sums_send, sums_send, sum_ss, sum_rs, other)
     totals_sent.wait_send()
     for j in (0, 1):
+        far_copy(j).wait_send()
+        product_copy(j).wait_send()
         for m in range(DIRECT_PIECES):
             direct_copy(j, m).wait_send()
     forward(3, h).wait_send()
@@ -463,7 +499,7 @@
     chunk_all.wait_send()
     inc_all.wait_send()
     handed.wait_send()
-    whole = remote(out_send, out_send, out_ss, out_rs, other)
+    whole = remote(done, done, out_ss, out_rs, other)
     whole.wait_send()
     whole.wait_recv()
 
@@ -477,14 +513,22 @@
     return pl.pallas_call(
         kernel,
         out_shape=pltpu.VMEM((256, 4096), BF16),
-        in_specs=[hbm, hbm, vmem, vmem, vmem, vmem, vmem, hbm, smem, smem],
+        in_specs=[hbm] * 8 + [smem, smem],
         out_specs=vmem,
         scratch_shapes=[
             V((1024, 1024), BF16),
             V((1024, 1024), BF16),
+            V((1024, 128), BF16),
+            V((1024, 128), BF16),
+            V((16, 1024), jnp.int32),
+            V((1, 1024), jnp.int32),
+            V((1, 1024), F32),
             V((4, 1024, 2048), BF16),
             V((4, 512, 1024), BF16),
             V((3, 256, 1024), BF16),
+            V((2, 256, 1024), BF16),
+            V((2, 512, 512), BF16),
+            V((2, 512, 512), BF16),
             V((2, 4, 16, 256), BF16),
             V((3, 16, 256), BF16),
             V((512, 2048), F32),
@@ -508,8 +552,8 @@
             V((8, 128, 128), BF16),
             V((256, 256), F32),
             V((1024, 1024), F32),
-            dma((2,)), dma, dma((3,)), dma((3,)),
-            dma((2, DIRECT_PIECES)), dma((2, DIRECT_PIECES)), dma((4, 4)), dma((4, 4)),
+            dma((7,)), dma, dma((3,)), dma((3,)),
+            dma((2, DIRECT_PIECES)), dma((2, DIRECT_PIECES)), dma((2,)), dma((2,)), dma((2,)), dma((2,)), dma((4, 5)), dma((4, 5)),
             dma, dma, dma, dma, dma, dma, dma, dma,
             dma((3,)), dma((3,)), dma, dma, dma((4,)), dma((4,)), dma, dma,
             dma, dma,

time: 77.8 us -> 74.4 us (0.956)
  Pallas kernels: 76.3 us -> 72.9 us
    pallas_call x1, Pallas kernels: 76.3 us -> 72.9 us  [local(): pl.pallas_call(kernel, out_shape=pltpu.VMEM((256, 4096), BF16), in_specs=...]
where the time goes in v3:
time: 74.4 us; the launch traced here: 74.3 us
  Pallas kernels  72.9 us (98%)
  local copies, waits for them, and re-layouts  1.32 us (2%)
    pallas_call x1, Pallas kernels, local(): pl.pallas_call(kernel, out_shape=pltpu.VMEM((256, 4096), BF16), in_specs=...  72.9 us

profile of v3, /device:TPU:1, one launch (start us, length us, event | category | flops | bytes accessed | tf_op | source)
XLA Modules:
  0.0 74.3 jit_solution(10807204746514261170)
XLA Ops:
  0.0 72.9 %shard_map.100 = bf16[256,4096]{1,0:T(8,128)(2,1)S(1)} custom-call(bf16[1024,1024]{1,0:T(8,128)(2,1)} %xs_hbm.1, bf16[1024,1024]{1,0:T(8,128)(2,1)} %gate_hbm.1, bf16[1024,128]{1,0:T(8,128)(2,1)} %bmat_hbm.1, bf16[1024,128]{1,0:T(8,128)(2,1)} %cmat_hbm.1, s32[16,1024]{1,0:T(8,128)} %dt_hbm.1, s32[1,1024]{1,0:T(1,128)} %bitcast.2, f32[1,1024]{1,0:T(1,128)} %bitcast.3, ...), custom_call_target="tpu_custom_call" | custom-call | tf_op jit(solution)/shard_map/pallas_call | solution.py:513
  72.9 1.3 %copy.12 = bf16[256,4096]{1,0:T(8,128)(2,1)} copy(bf16[256,4096]{1,0:T(8,128)(2,1)S(1)} %shard_map.100) | data formatting | bytes 4194304

commit v4 on v3

--- a/solution.py
+++ b/solution.py
@@ -49,6 +49,10 @@
             src_ref=src, dst_ref=dst, send_sem=ss, recv_sem=rs, device_id=dev, device_id_type=MESH
         )
 
+    base = c * 2048
+    own_weight = pltpu.make_async_copy(w_hbm.at[:, pl.ds(pl.multiple_of(base, 128), 2048)], weight.at[h], own_sem)
+    own_weight.start()
+
     barrier = pltpu.get_barrier_semaphore()
     chip = s // 2
 
@@ -84,15 +88,13 @@
     along = (at(x_a, z), at(x, z_a), at(x_b, z), at(x, z_b))
     bits = ((px, pz, ax, az), (pz, px, az, bx), (px, pz, bx, bz), (pz, px, bz, ax))
     mine = [b0 + 2 * b1 + 4 * b2 + 8 * b3 for b0, b1, b2, b3 in bits]
-    base = c * 2048
 
     def slice_send(j):
         for k in range(4):
             first, width = COLOURS[arrives_as[j]][k]
             rows = pl.ds(pl.multiple_of(mine[k] * 64, 64), 64)
-            src = w_hbm.at[rows, pl.ds(pl.multiple_of(base + first, 128), width)]
-            dst = weight.at[h, rows, pl.ds(first, width)]
-            remote(src, dst, slice_ss.at[j], slice_rs.at[arrives_as[j]], (s, planes[j])).start()
+            part = weight.at[h, rows, pl.ds(first, width)]
+            remote(part, part, slice_ss.at[j], slice_rs.at[arrives_as[j]], (s, planes[j])).start()
 
     def amount(t, j):
         return weight.at[planes[j], pl.ds(0, 64 << t), pl.ds(0, 2048 if j == 2 else 1280)]
@@ -105,9 +107,8 @@
 
     def direct_copy(j, m):
         rows = pl.ds(m * per, per)
-        src = w_hbm.at[rows, pl.ds(pl.multiple_of(base + 1280, 128), 256)]
-        dst = weight.at[h, rows, pl.ds(1280, 256)]
-        return remote(src, dst, direct_ss.at[j, m], direct_rs.at[1 - j, m], (s, planes[j]))
+        part = weight.at[h, rows, pl.ds(1280, 256)]
+        return remote(part, part, direct_ss.at[j, m], direct_rs.at[1 - j, m], (s, planes[j]))
 
     def direct_wait(j, m):
         part = weight.at[planes[j], pl.ds(m * per, per), pl.ds(1280, 256)]
@@ -140,10 +141,8 @@
             step_all(t - 1, j).wait_recv()
         step_send(t, j)
 
-    own_weight = pltpu.make_async_copy(w_hbm.at[:, pl.ds(pl.multiple_of(base, 128), 2048)], weight.at[h], own_sem)
-    own_weight.start()
-
     pl.semaphore_wait(barrier, 19)
+    own_weight.wait()
 
     slice_send(0)
     slice_send(1)
@@ -388,7 +387,6 @@
 
     forward(3, h).start()
 
-    own_weight.wait()
     for j in (0, 1):
         far_copy(j).wait_recv()
         for rows, value in ((here, hid_send), (there, hid_far)):
@@ -455,29 +453,37 @@
         for m in range(DIRECT_PIECES):
             direct_wait(j, m)
         acc[:, DIRECT] += jnp.dot(hid[planes[j]], weight[planes[j], :, DIRECT], preferred_element_type=F32)
+    def finish_part(n, colours):
+        offset, width = LAST[n]
+        spans = {k: slice(k * 512 + offset, k * 512 + offset + width) for k in colours}
+        columns = {k: pl.ds(pl.multiple_of(base + k * 512 + offset, 128), width) for k in colours}
+
+        def ended(rows, scale):
+            scale = jnp.concatenate([scale] * (width // 128), axis=1)
+            terms = {}
+            for k in colours:
+                depth = depth_of(k, True)
+                terms[k] = jnp.dot(hid[planes[2], rows, depth], weight[planes[2], depth, spans[k]], preferred_element_type=F32)
+            return {k: ((acc[rows, spans[k]] + terms[k]) * scale).astype(BF16) for k in colours}
+
+        for k, value in ended(there, scale_there).items():
+            done[:, spans[k]] = value
+        for k in colours:
+            remote(done.at[:, spans[k]], out.at[:, columns[k]], out_ss, out_rs, other).start()
+        for k, value in ended(here, scale_here).items():
+            out[:, columns[k]] = value
+
+    early, late = (0, 1, 2), (3,)
+    for n in (0, 1):
+        step_all(3, 2, n).wait_recv()
+        finish_part(n, early)
     for j in (0, 1):
         product_all(j).wait_recv()
     acc[:, PRODUCT] += product_recv[0].astype(F32) + product_recv[1].astype(F32)
-
-    for n, (offset, width) in enumerate(LAST):
-        step_all(3, 2, n).wait_recv()
-        spans = [slice(k * 512 + offset, k * 512 + offset + width) for k in range(4)]
-        columns = [pl.ds(pl.multiple_of(base + k * 512 + offset, 128), width) for k in range(4)]
-
-        def ended(rows, scale):
-            scale = jnp.concatenate([scale] * (width // 128), axis=1)
-            terms = []
-            for k in range(4):
-                depth = depth_of(k, True)
-                terms.append(jnp.dot(hid[planes[2], rows, depth], weight[planes[2], depth, spans[k]], preferred_element_type=F32))
-            return [((acc[rows, spans[k]] + terms[k]) * scale).astype(BF16) for k in range(4)]
-
-        for k, value in enumerate(ended(there, scale_there)):
-            done[:, spans[k]] = value
-        for k in range(4):
-            remote(done.at[:, spans[k]], out.at[:, columns[k]], out_ss, out_rs, other).start()
-        for k, value in enumerate(ended(here, scale_here)):
-            out[:, columns[k]] = value
+    for n in (0, 1):
+        finish_part(n, late)
+    step_all(3, 2, 2).wait_recv()
+    finish_part(2, early + late)
 
     for j in (0, 1, 2):
         slice_all(j).wait_send()

time: 74.4 us -> 72.8 us (0.978)
  Pallas kernels: 72.9 us -> 71.4 us
    pallas_call x1, Pallas kernels: 72.9 us -> 71.4 us  [local(): pl.pallas_call(kernel, out_shape=pltpu.VMEM((256, 4096), BF16), in_specs=...]
where the time goes in v4:
time: 72.8 us; the launch traced here: 72.7 us
  Pallas kernels  71.4 us (98%)
  local copies, waits for them, and re-layouts  1.32 us (2%)
    pallas_call x1, Pallas kernels, local(): pl.pallas_call(kernel, out_shape=pltpu.VMEM((256, 4096), BF16), in_specs=...  71.4 us

profile of v4, /device:TPU:1, one launch (start us, length us, event | category | flops | bytes accessed | tf_op | source)
XLA Modules:
  0.0 72.7 jit_solution(2731592183218745445)
XLA Ops:
  0.0 71.4 %shard_map.100 = bf16[256,4096]{1,0:T(8,128)(2,1)S(1)} custom-call(bf16[1024,1024]{1,0:T(8,128)(2,1)} %xs_hbm.1, bf16[1024,1024]{1,0:T(8,128)(2,1)} %gate_hbm.1, bf16[1024,128]{1,0:T(8,128)(2,1)} %bmat_hbm.1, bf16[1024,128]{1,0:T(8,128)(2,1)} %cmat_hbm.1, s32[16,1024]{1,0:T(8,128)} %dt_hbm.1, s32[1,1024]{1,0:T(1,128)} %bitcast.2, f32[1,1024]{1,0:T(1,128)} %bitcast.3, ...), custom_call_target="tpu_custom_call" | custom-call | tf_op jit(solution)/shard_map/pallas_call | solution.py:519
  71.4 1.3 %copy.12 = bf16[256,4096]{1,0:T(8,128)(2,1)} copy(bf16[256,4096]{1,0:T(8,128)(2,1)S(1)} %shard_map.100) | data formatting | bytes 4194304

commit v5 on v4

--- a/solution.py
+++ b/solution.py
@@ -30,9 +30,9 @@
 
 
 def kernel(
-    xs_hbm, gate_hbm, bmat_hbm, cmat_hbm, dt_hbm, resets_hbm, gain_hbm, w_hbm, rate, skip,
+    xs_hbm, gate_hbm, bmat_hbm, cmat_hbm, dt_hbm, resets_hbm, gain_hbm, w_hbm, rate_hbm, skip_hbm,
     out,
-    xs, gate, bmat, cmat, dt, resets, gain, weight, hid, hid_send, hid_far, product_send, product_recv, sums, sums_send, acc, done,
+    rate, skip, xs, gate, bmat, cmat, dt, resets, gain, weight, hid, hid_send, hid_far, product_send, product_recv, sums, sums_send, acc, done,
     tri, col, split, bt, cjp, cntrow, grow, starts, reach, whole_send, pair_recv, chunk_send, chunk_recv, inc_send, inc_recv,
     pair_out, incoming, cbm, local,
     in_sem, own_sem, slice_ss, slice_rs, direct_ss, direct_rs, far_ss, far_rs, product_ss, product_rs, step_ss, step_rs,
@@ -67,8 +67,8 @@
     for d in (1, 2, 3):
         pl.semaphore_signal(barrier, inc=1, device_id=(s, (h + d) % 4), device_id_type=MESH)
 
-    sources = (dt_hbm, resets_hbm, bmat_hbm, cmat_hbm, xs_hbm, gate_hbm, gain_hbm)
-    places = (dt, resets, bmat, cmat, xs, gate, gain)
+    sources = (dt_hbm, resets_hbm, bmat_hbm, cmat_hbm, xs_hbm, gate_hbm, gain_hbm, rate_hbm, skip_hbm)
+    places = (dt, resets, bmat, cmat, xs, gate, gain, rate, skip)
     copies_in = [pltpu.make_async_copy(a, b, in_sem.at[n]) for n, (a, b) in enumerate(zip(sources, places))]
     for cp in copies_in:
         cp.start()
@@ -148,7 +148,7 @@
     slice_send(1)
 
     tri[...] = jnp.where(iota((SPAN, SPAN), 0) <= iota((SPAN, SPAN), 1), 1.0, 0.0).astype(BF16)
-    for n in (0, 1, 2):
+    for n in (0, 1, 2, 7, 8):
         copies_in[n].wait()
     head_row = iota((16, SPAN), 0)
     slope = jnp.zeros((16, SPAN), F32)
@@ -182,7 +182,7 @@
     def in_parts(row):
         high = row.astype(BF16).astype(F32)
         mid = (row - high).astype(BF16).astype(F32)
-        line = iota((16, 128), 0)
+        line = iota((8, 128), 0)
         low = row - high - mid
         return jnp.where(line == 0, high, jnp.where(line == 1, mid, jnp.where(line == 2, low, 0.0))).astype(BF16)
 
@@ -215,7 +215,7 @@
                 run = through * run + fresh[q, b]
                 product = product * through
             whole_send[q, 0:128, :] = run.astype(BF16)
-            whole_send[q, 128:144, :] = in_parts(product)
+            whole_send[q, 128:136, :] = in_parts(product)
 
     for q in range(0, 8, 2):
         states((q, q + 1))
@@ -257,7 +257,7 @@
     first_core = c == 0
     for n in range(4):
         own, far = whole_send[4 * c + n], pair_recv[n]
-        own_through, far_through = from_parts(own[128:144]), from_parts(far[128:144])
+        own_through, far_through = from_parts(own[128:136]), from_parts(far[128:136])
         own_state, far_state = own[0:128].astype(F32), far[0:128].astype(F32)
         earlier = jnp.where(first_core, own_state, far_state)
         later = jnp.where(first_core, far_state, own_state)
@@ -265,7 +265,7 @@
         tail = in_parts(own_through * far_through)
         for r in range(4):
             chunk_send[n * 4 + r, 0:32, :] = total[r * 32:(r + 1) * 32].astype(BF16)
-            chunk_send[n * 4 + r, 32:48, :] = tail
+            chunk_send[n * 4 + r, 32:40, :] = tail
 
     @pl.loop(1, 16)
     def _(i):
@@ -290,7 +290,7 @@
     state = jnp.zeros((32, 128), F32)
     for t in range(16):
         inc_send[t] = state.astype(BF16)
-        state = from_parts(chunk_recv[t, 32:48, :]) * state + chunk_recv[t, 0:32, :].astype(F32)
+        state = from_parts(chunk_recv[t, 32:40, :]) * state + chunk_recv[t, 0:32, :].astype(F32)
 
     @pl.loop(1, 16)
     def _(i):
@@ -309,7 +309,7 @@
     for n in range(4):
         own, far = whole_send[4 * c + n], pair_recv[n]
         first_state = jnp.where(first_core, own[0:128].astype(F32), far[0:128].astype(F32))
-        first_through = jnp.where(first_core, from_parts(own[128:144]), from_parts(far[128:144]))
+        first_through = jnp.where(first_core, from_parts(own[128:136]), from_parts(far[128:136]))
         reaching = inc_recv[n * 4:(n + 1) * 4].reshape(STATE, 128)
         second = (first_through * reaching.astype(F32) + first_state).astype(BF16)
         incoming[4 * c + n] = jnp.where(first_core, reaching.astype(F32), second.astype(F32)).astype(BF16)
@@ -513,15 +513,16 @@
 def local(xs, gate_branch, bmat, cmat, dt_code, resets, decay_rate, skip, norm_gain, out_weight):
     vmem = pl.BlockSpec(memory_space=pltpu.VMEM)
     hbm = pl.BlockSpec(memory_space=pl.ANY)
-    smem = pl.BlockSpec(memory_space=pltpu.SMEM)
     dma = pltpu.SemaphoreType.DMA
     V = pltpu.VMEM
     return pl.pallas_call(
         kernel,
         out_shape=pltpu.VMEM((256, 4096), BF16),
-        in_specs=[hbm] * 8 + [smem, smem],
+        in_specs=[hbm] * 10,
         out_specs=vmem,
         scratch_shapes=[
+            pltpu.SMEM((16,), F32),
+            pltpu.SMEM((16,), F32),
             V((1024, 1024), BF16),
             V((1024, 1024), BF16),
             V((1024, 128), BF16),
@@ -548,17 +549,17 @@
             V((1024, 1024), F32),
             V((4, 8, 128, 128), F32),
             V((4, 8, 8, 128), F32),
-            V((8, 144, 128), BF16),
-            V((4, 144, 128), BF16),
-            V((16, 48, 128), BF16),
-            V((16, 48, 128), BF16),
+            V((8, 136, 128), BF16),
+            V((4, 136, 128), BF16),
+            V((16, 40, 128), BF16),
+            V((16, 40, 128), BF16),
             V((16, 32, 128), BF16),
             V((16, 32, 128), BF16),
             V((4, 128, 128), BF16),
             V((8, 128, 128), BF16),
             V((256, 256), F32),
             V((1024, 1024), F32),
-            dma((7,)), dma, dma((3,)), dma((3,)),
+            dma((9,)), dma, dma((3,)), dma((3,)),
             dma((2, DIRECT_PIECES)), dma((2, DIRECT_PIECES)), dma((2,)), dma((2,)), dma((2,)), dma((2,)), dma((4, 5)), dma((4, 5)),
             dma, dma, dma, dma, dma, dma, dma, dma,
             dma((3,)), dma((3,)), dma, dma, dma((4,)), dma((4,)), dma, dma,

time: 72.8 us -> 72 us (0.989)
  Pallas kernels: 71.4 us -> 70.6 us
    pallas_call x1, Pallas kernels: 71.4 us -> 70.6 us  [local(): pl.pallas_call(kernel, out_shape=pltpu.VMEM((256, 4096), BF16), in_specs=...]
where the time goes in v5:
time: 72 us; the launch traced here: 71.9 us
  Pallas kernels  70.6 us (98%)
  local copies, waits for them, and re-layouts  1.32 us (2%)
    pallas_call x1, Pallas kernels, local(): pl.pallas_call(kernel, out_shape=pltpu.VMEM((256, 4096), BF16), in_specs=...  70.6 us

profile of v5, /device:TPU:1, one launch (start us, length us, event | category | flops | bytes accessed | tf_op | source)
XLA Modules:
  0.0 71.9 jit_solution(17802046876392891504)
XLA Ops:
  0.0 70.6 %shard_map.100 = bf16[256,4096]{1,0:T(8,128)(2,1)S(1)} custom-call(bf16[1024,1024]{1,0:T(8,128)(2,1)} %xs_hbm.1, bf16[1024,1024]{1,0:T(8,128)(2,1)} %gate_hbm.1, bf16[1024,128]{1,0:T(8,128)(2,1)} %bmat_hbm.1, bf16[1024,128]{1,0:T(8,128)(2,1)} %cmat_hbm.1, s32[16,1024]{1,0:T(8,128)} %dt_hbm.1, s32[1,1024]{1,0:T(1,128)} %bitcast.2, f32[1,1024]{1,0:T(1,128)} %bitcast.3, ...), custom_call_target="tpu_custom_call" | custom-call | tf_op jit(solution)/shard_map/pallas_call | solution.py:518
  70.6 1.3 %copy.12 = bf16[256,4096]{1,0:T(8,128)(2,1)} copy(bf16[256,4096]{1,0:T(8,128)(2,1)S(1)} %shard_map.100) | data formatting | bytes 4194304
